TPU v7x, 128 devices: a whole 4x4x4 slice. The times are simulated.
128 devices in a mesh: rows: 16 (over z, y), cols: 8 (over x, core).
Axes of the slice: x: 4, y: 4, z: 4, core: 2. Of those that a mesh axis runs over, the one named last changes fastest.
Arguments:
- train_query: bfloat16 [8192, 8192], P('rows', 'cols'), may hold values from -0.0625 to 0.0625
- low_query: bfloat16 [8192, 64], P('rows'), may hold values from -0.0625 to 0.0625
- high_query: bfloat16 [64, 8192], P(None, 'cols'), may hold values from -0.75 to 0.75
- train_key: bfloat16 [8192, 512], P('rows', 'cols'), may hold values from -0.0625 to 0.0625
- low_key: bfloat16 [8192, 64], P('rows'), may hold values from -0.0625 to 0.0625
- high_key: bfloat16 [64, 512], P(None, 'cols'), may hold values from -0.75 to 0.75
- train_value: bfloat16 [8192, 512], P('rows', 'cols'), may hold values from -0.0625 to 0.0625
- low_value: bfloat16 [8192, 64], P('rows'), may hold values from -0.0625 to 0.0625
- high_value: bfloat16 [64, 512], P(None, 'cols'), may hold values from -0.75 to 0.75
- norm_train: float32 [8192], P(('rows', 'cols')), may hold values from 0.25 to 1.75
- norm_step: float32 [8192], P(('rows', 'cols')), may hold values from -0.3 to 0.3
Outputs:
- serving_query: bfloat16 [8192, 8192], P('cols')
- serving_key: bfloat16 [512, 8192], P('cols')
- serving_value: bfloat16 [512, 8192], P('cols')
- serve_norm: bfloat16 [8192], replicated
All inputs are finite; a program needn't handle non-finite values.
Results may differ from a plain program's by a relative error of at most 0.001.
Values may be sent and summed in bfloat16 or wider, within the bound.
No kernel may reach another device: no remote copies, remote signals or barrier semaphores. Data moves between devices by JAX's collectives and lax.ppermute only.
A program may use at most 128 MiB of HBM per device.

v0:
```python
import jax
import jax.numpy as jnp
from jax import lax
from jax.sharding import PartitionSpec as P

mix_rate = 1.0


def side_by_side(arrays, axis, dim, along):
    both = jnp.concatenate(arrays, axis=along)
    out, at, finished = (lax.all_gather(both, axis, axis=dim, tiled=True), 0, [])
    for a in arrays:
        finished.append(lax.slice_in_dim(out, at, at + a.shape[along], axis=along))
        at += a.shape[along]
    return tuple(finished)


def body(
    train_query,
    low_query,
    high_query,
    train_key,
    low_key,
    high_key,
    train_value,
    low_value,
    high_value,
    norm_train,
    norm_step,
):
    whole_query = train_query.astype(jnp.float32) + mix_rate * jnp.dot(
        low_query, high_query, preferred_element_type=jnp.float32
    )
    whole_key = train_key.astype(jnp.float32) + mix_rate * jnp.dot(
        low_key, high_key, preferred_element_type=jnp.float32
    )
    whole_value = train_value.astype(jnp.float32) + mix_rate * jnp.dot(
        low_value, high_value, preferred_element_type=jnp.float32
    )
    narrow_query, narrow_key, narrow_value = (
        whole_query.astype(jnp.bfloat16),
        whole_key.astype(jnp.bfloat16),
        whole_value.astype(jnp.bfloat16),
    )
    serving_query, serving_key, serving_value = side_by_side(
        (narrow_query, narrow_key, narrow_value), "rows", 0, 1
    )
    serving_query, serving_key, serving_value = (serving_query.T, serving_key.T, serving_value.T)
    serve_norm = lax.all_gather(
        (norm_train + norm_step).astype(jnp.bfloat16), ("rows", "cols"), axis=0, tiled=True
    )
    return (serving_query, serving_key, serving_value, serve_norm)


def solution(mesh):
    return jax.shard_map(
        body,
        mesh=mesh,
        in_specs=(
            P("rows", "cols"),
            P("rows", None),
            P(None, "cols"),
            P("rows", "cols"),
            P("rows", None),
            P(None, "cols"),
            P("rows", "cols"),
            P("rows", None),
            P(None, "cols"),
            P(("rows", "cols")),
            P(("rows", "cols")),
        ),
        out_specs=(P("cols", None), P("cols", None), P("cols", None), P()),
        check_vma=False,
    )
```

profile of v0, /device:TPU:1, one launch (start us, length us, event | category | flops | bytes accessed | tf_op | source)
XLA Modules:
  0.0 190.5 jit_solution(3674972838845907231)
XLA Ops:
  7.2 0.0 copy-start
  7.2 0.0 all-gather.2.cloned.1.call-start
  7.2 1.1 fusion
  8.3 0.1 copy.22
  8.5 1.1 fusion.1
  9.6 0.1 copy.23
  9.7 0.0 copy-done
  9.7 1.7 add_convert_fusion
  11.4 0.0 copy-start.1
  11.4 0.0 copy-start.2
  11.5 1.9 %concatenate.3 = bf16[512,1152]{1,0:T(8,128)(2,1)} concatenate(bf16[512,1024]{1,0:T(8,128)(2,1)S(1)} %add_convert_fusion, bf16[512,64]{1,0:T(8,128)(2,1)S(1)} %copy.22, bf16[512,64]{1,0:T(8,128)(2,1)S(1)} %copy.23), dimensions={1} | concatenate | bytes 2359296 | tf_op jit(solution)/shard_map/concatenate | solution.py:10
  13.4 0.0 all-gather.2.cloned.1.call-update
  13.4 0.0 copy-done.1
  13.4 0.0 copy-done.2
  13.5 0.2 dynamic-update-slice
  13.7 71.5 %all-reduce = bf16[8192]{0:T(1024)(128)(2,1)} all-reduce(bf16[8192]{0:T(1024)(128)(2,1)S(1)} %dynamic-update-slice), channel_id=1, replica_groups=mesh['rows'=16,'cols'=8] {'rows','cols'}, use_global_device_ids=true, to_apply=%add | all-reduce | flops 8192 | bytes 32768
  85.3 54.5 %all-gather.2.cloned.1.call-done = bf16[8192,1152]{1,0:T(8,128)(2,1)} async-done(((bf16[512,1152]{1,0:T(8,128)(2,1)}), bf16[8192,1152]{1,0:T(8,128)(2,1)}) %all-gather.2.cloned.1.call-update) | async-done | bytes 18874384 | tf_op jit(solution)/shard_map/all_gather | solution.py:11
  139.8 4.6 %slice_bitcast_fusion.1 = (bf16[64,8192]{0,1:T(8,128)(2,1)S(1)}, bf16[64,8192]{0,1:T(8,128)(2,1)}) fusion(bf16[8192,1152]{1,0:T(8,128)(2,1)} %all-gather.2.cloned.1.call-done), kind=kLoop, calls=%fused_computation.1 | loop fusion | bytes 4194304 | tf_op jit(solution)/shard_map/transpose | solution.py:48
  144.3 2.7 %copy.25 = bf16[64,8192]{1,0:T(8,128)(2,1)} copy(bf16[64,8192]{0,1:T(8,128)(2,1)} %get-tuple-element.13) | data formatting | bytes 2097152
  147.0 1.6 copy.26
  148.6 13.9 %slice_bitcast_fusion = bf16[1024,8192]{0,1:T(8,128)(2,1)} fusion(bf16[8192,1152]{1,0:T(8,128)(2,1)} %all-gather.2.cloned.1.call-done), kind=kLoop, calls=%fused_computation | loop fusion | bytes 33554432 | tf_op jit(solution)/shard_map/transpose | solution.py:48
  162.5 21.2 %copy.24 = bf16[1024,8192]{1,0:T(8,128)(2,1)} copy(bf16[1024,8192]{0,1:T(8,128)(2,1)} %slice_bitcast_fusion) | data formatting | bytes 33554432
  (2 shorter events, 0.0 us)
Async XLA Ops:
  7.2 2.5 %copy-start = (bf16[64,1024]{1,0:T(8,128)(2,1)S(1)}, bf16[64,1024]{1,0:T(8,128)(2,1)}, u32[]{:S(2)}) copy-start(bf16[64,1024]{1,0:T(8,128)(2,1)} %param.13) | copy-start | bytes 393220
  7.2 132.6 %all-gather.2.cloned.1.call-start = ((), (), s32[]{:S(2)}) async-start(), calls=%async_computation | async-start | bytes 20054016 | tf_op jit(solution)/shard_map/all_gather | solution.py:11
  11.4 2.0 %copy-start.1 = (f32[64]{0:T(128)S(1)}, f32[64]{0:T(128)}, u32[]{:S(2)}) copy-start(f32[64]{0:T(128)} %param.20) | copy-start | bytes 772
  11.4 2.0 %copy-start.2 = (f32[64]{0:T(128)S(1)}, f32[64]{0:T(128)}, u32[]{:S(2)}) copy-start(f32[64]{0:T(128)} %param.21) | copy-start | bytes 772
Sparse Core Ops, SparseCore 0:
  13.5 126.1 all-gather.1
where the time goes:
time: 191 us
  blocking collectives  71.5 us (37%)
  waiting for transfers between devices  54.5 us (29%)
  local copies, waits for them, and re-layouts  46.4 us (24%)
  between operations  14.1 us (7%)
  matrix products  3.93 us (2%)
    unnamed x1, blocking collectives  71.5 us
    all_gather x1, waiting for transfers between devices, side_by_side(): lax.all_gather(both, axis, axis=dim, tiled=True)  54.5 us
    unnamed x11, local copies, waits for them, and re-layouts  25.8 us
    transpose x2, local copies, waits for them, and re-layouts, body(): serving_query, serving_key, serving_value = (serving_query.T, serving_key...  18.4 us
  transfers between devices with their start and end apart: 1, of which 1 were waited for; matrix products, arithmetic and copies ran while one was open for 0% of the time, Pallas kernels for 0%

commit v1 on v0

v1 whole, which is shorter than its diff:
```python
import functools
import jax
import jax.numpy as jnp
from jax import lax
from jax.experimental import pallas as pl
from jax.experimental.pallas import tpu as pltpu
from jax.sharding import PartitionSpec as P


mix_rate = 1.0


SIDE = 4
CORES = 2
STEP = 128
CHUNK = 256
MERGE_VMEM = 65_860_000
PARTS = 2


def merge_kernel(*refs):
    out, held, sem = refs[9], refs[10:-1], refs[-1]
    train, low, high, key, low_key, high_key, value, low_value, high_value = held
    rows, wide = train.shape
    parts = [pl.ds(at, STEP) for at in range(0, rows, STEP)]
    rest = len(parts)
    copies = [pltpu.make_async_copy(refs[0].at[part], train.at[part], sem.at[i]) for i, part in enumerate(parts)]
    copies += [pltpu.make_async_copy(refs[i], held[i], sem.at[rest + i - 1]) for i in range(1, 9)]
    order = [rest, rest + 1, *range(rest), *range(rest + 2, rest + 8)]
    for i in order:
        copies[i].start()

    def product(left, right):
        return lax.dot_general(right, left, (((0,), (0,)), ((), ())), preferred_element_type=jnp.float32)

    copies[rest].wait()
    copies[rest + 1].wait()
    for copy, part in zip(copies, parts):
        copy.wait()
        for at in range(0, wide, CHUNK):
            base = train[part, at : at + CHUNK].T.astype(jnp.float32)
            whole = base + mix_rate * product(low[:, part], high[:, at : at + CHUNK])
            out[at : at + CHUNK, part] = whole.astype(jnp.bfloat16)
    for copy in copies[rest + 2 :]:
        copy.wait()
    at = wide
    for base, left, right in ((key, low_key, high_key), (value, low_value, high_value)):
        whole = base[...].astype(jnp.float32) + mix_rate * product(left[...], right[...])
        out[at : at + base.shape[0], :] = whole.astype(jnp.bfloat16)
        at += base.shape[0]


def merged(train, low, high, train_key, low_key, high_key, train_value, low_value, high_value):
    rows, columns = train.shape
    total = columns + train_key.shape[1] + train_value.shape[1]
    small = (low.T, high, train_key.T, low_key.T, high_key, train_value.T, low_value.T, high_value)
    return pl.pallas_call(
        merge_kernel,
        in_specs=[pl.BlockSpec(memory_space=pltpu.HBM)] * 9,
        out_specs=pl.BlockSpec(memory_space=pltpu.VMEM),
        out_shape=jax.ShapeDtypeStruct((total, rows), jnp.bfloat16),
        scratch_shapes=[
            pltpu.VMEM(train.shape, train.dtype),
            *[pltpu.VMEM(x.shape, x.dtype) for x in small],
            pltpu.SemaphoreType.DMA((8 + rows // STEP,)),
        ],
        compiler_params=pltpu.CompilerParams(vmem_limit_bytes=MERGE_VMEM),
        cost_estimate=pl.CostEstimate(flops=10**8, bytes_accessed=10**7, transcendentals=0),
        name="merge",
    )(train, *small)


def place_kernel(plan, *refs):
    count = len(plan)
    pieces = refs[:count]
    outs, held, into, out_of = refs[-count - 5 : -count - 2], refs[-count - 2 : -2], refs[-2], refs[-1]
    rank = lax.axis_index("rows")
    first_axis_is_y = lax.rem(lax.axis_index("cols"), CORES) == 0
    y, z = lax.rem(rank, SIDE), lax.div(rank, SIDE)
    reads, writes = [], []
    for piece, kept, (first, one, two) in zip(pieces, held, plan):
        dy, dz = jnp.where(first_axis_is_y, one, two), jnp.where(first_axis_is_y, two, one)
        origin = lax.rem(z + dz, SIDE) * SIDE + lax.rem(y + dy, SIDE)
        width = piece.shape[1]
        at = pl.ds(pl.multiple_of(origin * width, width), width)
        half = piece.shape[0] // PARTS
        for part in range(PARTS):
            low, high = part * half, (part + 1) * half
            reads.append(
                pltpu.make_async_copy(piece.at[pl.ds(low, half)], kept.at[pl.ds(low, half)], into.at[len(reads)])
            )
            group, start = [], 0
            for out in outs:
                stop = start + out.shape[0]
                begin, end = max(start, first + low), min(stop, first + high)
                if begin < end:
                    group.append((kept.at[pl.ds(begin - first, end - begin)], out.at[pl.ds(begin - start, end - begin), at]))
                start = stop
            writes.append(group)
    for read in reads:
        read.start()
    started = []
    for read, group in zip(reads, writes):
        read.wait()
        for source, target in group:
            started.append(pltpu.make_async_copy(source, target, out_of.at[len(started)]))
            started[-1].start()
    for copy in started:
        copy.wait()


def place(pieces, plan, outs, shapes):
    count = len(pieces)
    hbm = pl.BlockSpec(memory_space=pltpu.HBM)
    given = () if outs is None else outs
    return pl.pallas_call(
        functools.partial(place_kernel, tuple(plan)),
        in_specs=[hbm] * (count + len(given)),
        out_specs=[hbm] * 3,
        out_shape=shapes,
        scratch_shapes=[
            *[pltpu.VMEM(p.shape, p.dtype) for p in pieces],
            pltpu.SemaphoreType.DMA((PARTS * count,)),
            pltpu.SemaphoreType.DMA((PARTS * count + 3 * count,)),
        ],
        input_output_aliases={count + i: i for i in range(len(given))},
        compiler_params=pltpu.CompilerParams(vmem_limit_bytes=5 << 20),
        cost_estimate=pl.CostEstimate(
            flops=10**6, bytes_accessed=4 * sum(p.size for p in pieces), transcendentals=0
        ),
        name="place",
    )(*pieces, *given)


def along(second, by):
    pairs = []
    for z in range(SIDE):
        for y in range(SIDE):
            for x in range(SIDE):
                for core in range(CORES):
                    on_z = (core == 1) != second
                    to_z, to_y = ((z + by) % SIDE, y) if on_z else (z, (y + by) % SIDE)
                    flat = lambda r, q: ((r * SIDE + q) * SIDE + x) * CORES + core
                    pairs.append((flat(z, y), flat(to_z, to_y)))
    return pairs


def exchange(mine, bit, swapped):
    count = SIDE * SIDE * SIDE * CORES
    pick = lambda i: swapped if i % CORES else bit
    other = lax.ppermute(mine, ("rows", "cols"), [(i, i ^ pick(i)) for i in range(count)])
    index = lax.axis_index(("rows", "cols"))
    mask = jnp.where(index % CORES == 0, bit, swapped)
    return jnp.where((index & mask) == 0, jnp.concatenate([mine, other]), jnp.concatenate([other, mine]))


def in_order(norm):
    four = norm.reshape(SIDE, SIDE, SIDE, -1)
    on_y = lax.axis_index("cols") % CORES == 0
    return jnp.where(on_y, four.transpose(2, 0, 1, 3), four.transpose(0, 2, 1, 3)).reshape(-1)


def body(
    train_query,
    low_query,
    high_query,
    train_key,
    low_key,
    high_key,
    train_value,
    low_value,
    high_value,
    norm_train,
    norm_step,
):
    shapes = [
        jax.ShapeDtypeStruct((w.shape[1], w.shape[0] * SIDE * SIDE), jnp.bfloat16)
        for w in (train_query, train_key, train_value)
    ]
    own = merged(train_query, low_query, high_query, train_key, low_key, high_key, train_value, low_value, high_value)
    part = own.shape[0] // 2

    def one(x, by):
        return lax.ppermute(x, ("rows", "cols"), along(False, by))

    def two(x, by):
        return lax.ppermute(x, ("rows", "cols"), along(True, by))

    outs = None

    def put(pieces, plan):
        nonlocal outs
        outs = place(pieces, plan, outs, shapes)

    a_up, a_down = one(own, 1), one(own, -1)
    norm = (norm_train + norm_step).astype(jnp.bfloat16)
    norm = exchange(norm, 1, 1)
    norm = exchange(norm, 32, 8)
    norm = exchange(norm, 64, 16)
    c_up, c_down = two(own, 1), two(own, -1)
    norm = exchange(norm, 2, 2)
    put([own], [(0, 0, 0)])
    norm = exchange(norm, 4, 4)
    b = one(a_up, 1)
    d_down = two(a_up, -1)
    g_down = two(a_down, -1)
    put([a_up, a_down], [(0, 3, 0), (0, 1, 0)])
    far = two(c_up, 1)
    put([c_up, c_down], [(0, 0, 3), (0, 0, 1)])
    d_up = two(a_up, 1)
    g_up = two(a_down, 1)
    norm = exchange(norm, 8, 32)
    e_down, e_up = two(b, -1), two(b, 1)
    g_far = two(g_down, -1)
    put([b, d_down], [(0, 2, 0), (0, 3, 1)])
    norm = exchange(norm, 16, 64)
    d_far_low = two(d_down[part:], -1)
    e_far = two(e_down, -1)
    put([far, g_down], [(0, 0, 2), (0, 1, 1)])
    d_far_top = two(d_up[:part], 1)
    put([d_up, e_down], [(0, 3, 3), (0, 2, 1)])
    serve_norm = in_order(norm)
    put([g_up, g_far], [(0, 1, 3), (0, 1, 2)])
    put([e_up, e_far], [(0, 2, 3), (0, 2, 2)])
    put([d_far_top, d_far_low], [(0, 3, 2), (part, 3, 2)])
    return (*outs, serve_norm)


def solution(mesh):
    return jax.shard_map(
        body,
        mesh=mesh,
        in_specs=(
            P("rows", "cols"),
            P("rows", None),
            P(None, "cols"),
            P("rows", "cols"),
            P("rows", None),
            P(None, "cols"),
            P("rows", "cols"),
            P("rows", None),
            P(None, "cols"),
            P(("rows", "cols")),
            P(("rows", "cols")),
        ),
        out_specs=(P("cols", None), P("cols", None), P("cols", None), P()),
        check_vma=False,
    )
```

time: 191 us -> 144 us (0.75)
  the two profiles are of different devices: /device:TPU:1 before, /device:TPU:0 now
where the time goes in v1:
time: 144 us
  waiting for transfers between devices  71.8 us (50%)
  starting transfers between devices  44.2 us (31%)
  Pallas kernels  24 us (17%)
  local copies, waits for them, and re-layouts  3.09 us (2%)
    ppermute x13, waiting for transfers between devices, two(): return lax.ppermute(x, ('rows', 'cols'), along(True, by))  44 us
    ppermute x13, starting transfers between devices, two(): return lax.ppermute(x, ('rows', 'cols'), along(True, by))  22.7 us
    pallas_call x9, Pallas kernels, place(): pl.pallas_call(functools.partial(place_kernel, tuple(plan)), in_specs=[hb...  20.5 us
    ppermute x3, waiting for transfers between devices, one(): return lax.ppermute(x, ('rows', 'cols'), along(False, by))  18.9 us
    ppermute x7, starting transfers between devices, exchange(): lax.ppermute(mine, ('rows', 'cols'), [(i, i ^ pick(i)) for i in range(cou...  17.5 us
    ppermute x7, waiting for transfers between devices, exchange(): lax.ppermute(mine, ('rows', 'cols'), [(i, i ^ pick(i)) for i in range(cou...  8.87 us
    ppermute x3, starting transfers between devices, one(): return lax.ppermute(x, ('rows', 'cols'), along(False, by))  3.98 us
    pallas_call x1, Pallas kernels, merged(): pl.pallas_call(merge_kernel, in_specs=[pl.BlockSpec(memory_space=pltpu.HB...  3.47 us
  transfers between devices with their start and end apart: 23, of which 11 were waited for; matrix products, arithmetic and copies ran while one was open for 1% of the time, Pallas kernels for 13%

profile of v1, /device:TPU:0, one launch (start us, length us, event | category | flops | bytes accessed | tf_op | source)
XLA Modules:
  0.0 144.1 jit_solution(4094170849651564870)
XLA Ops:
  0.7 3.5 %merge.1.refs_0_ = bf16[1152,512]{1,0:T(8,128)(2,1)} custom-call(bf16[512,1024]{1,0:T(8,128)(2,1)} %refs_0_.1, bf16[64,512]{1,0:T(8,128)(2,1)} %bitcast.17, bf16[64,1024]{1,0:T(8,128)(2,1)} %refs_2_.1, bf16[64,512]{1,0:T(8,128)(2,1)} %bitcast.18, bf16[64,512]{1,0:T(8,128)(2,1)} %bitcast.19, bf16[64,64]{1,0:T(8,128)(2,1)} %refs_5_.1, ...), custom_call_target="tpu_custom_call" | custom-call | flops 100000000 | bytes 10000000 | tf_op jit(solution)/shard_map/merge/pallas_call | solution.py:57
  4.1 1.8 %collective-permute-start = (bf16[1152,512]{1,0:T(8,128)(2,1)}, bf16[1152,512]{1,0:T(8,128)(2,1)}, u32[]{:S(2)}, u32[]{:S(2)}) collective-permute-start(bf16[1152,512]{1,0:T(8,128)(2,1)} %merge.1.refs_0_), channel_id=1, source_target_pairs={{0,8},{1,33},{2,10},{3,35},{4,12},{5,37},{6,14},{7,39},{8,16},{9,4... | collective-permute-start | bytes 3538952 | tf_op jit(solution)/shard_map/ppermute | solution.py:184
  5.9 1.5 %collective-permute-start.9 = (bf16[1152,512]{1,0:T(8,128)(2,1)}, bf16[1152,512]{1,0:T(8,128)(2,1)}, u32[]{:S(2)}, u32[]{:S(2)}) collective-permute-start(bf16[1152,512]{1,0:T(8,128)(2,1)} %merge.1.refs_0_), channel_id=1, source_target_pairs={{0,24},{1,97},{2,26},{3,99},{4,28},{5,101},{6,30},{7,103},{8,0},{9... | collective-permute-start | bytes 3538952 | tf_op jit(solution)/shard_map/ppermute | solution.py:184
  7.4 2.0 %collective-permute-start.13 = (bf16[1152,512]{1,0:T(8,128)(2,1)}, bf16[1152,512]{1,0:T(8,128)(2,1)S(1)}, u32[]{:S(2)}, u32[]{:S(2)}) collective-permute-start(bf16[1152,512]{1,0:T(8,128)(2,1)} %merge.1.refs_0_), channel_id=1, source_target_pairs={{0,32},{1,9},{2,34},{3,11},{4,36},{5,13},{6,38},{7,15},{8,40},{9,1... | collective-permute-start | bytes 3538952 | tf_op jit(solution)/shard_map/ppermute | solution.py:187
  9.5 0.1 collective-permute-start.16
  9.6 1.1 collective-permute-done.16
  10.7 0.1 broadcast_select_fusion
  10.8 1.9 %collective-permute-start.17 = (bf16[128]{0:T(256)(128)(2,1)S(1)}, bf16[128]{0:T(256)(128)(2,1)S(1)}, u32[]{:S(2)}, u32[]{:S(2)}) collective-permute-start(bf16[128]{0:T(256)(128)(2,1)S(1)} %broadcast_select_fusion), channel_id=1, source_target_pairs={{0,32},{1,9},{2,34},{3,11},{4,36},{5,13},{6,38},{7,15},{8,40},{9,1... | collective-permute-start | bytes 776 | tf_op jit(solution)/shard_map/ppermute | solution.py:151
  12.7 18.9 %collective-permute-done.refs_0_ = bf16[1152,512]{1,0:T(8,128)(2,1)} collective-permute-done((bf16[1152,512]{1,0:T(8,128)(2,1)}, bf16[1152,512]{1,0:T(8,128)(2,1)}, u32[]{:S(2)}, u32[]{:S(2)}) %collective-permute-start) | collective-permute-done | bytes 1179680 | tf_op jit(solution)/shard_map/ppermute | solution.py:184
  31.7 0.7 collective-permute-start.5
  32.4 6.3 %collective-permute-start.18 = (bf16[256]{0:T(256)(128)(2,1)S(1)}, bf16[256]{0:T(256)(128)(2,1)S(1)}, u32[]{:S(2)}, u32[]{:S(2)}) collective-permute-start(bf16[256]{0:T(256)(128)(2,1)S(1)} %broadcast_select_fusion.1), channel_id=1, source_target_pairs={{0,64},{1,17},{2,66},{3,19},{4,68},{5,21},{6,70},{7,23},{8,72},{9,... | collective-permute-start | bytes 1544 | tf_op jit(solution)/shard_map/ppermute | solution.py:151
  38.7 1.6 %collective-permute-done.18 = bf16[256]{0:T(256)(128)(2,1)S(1)} collective-permute-done((bf16[256]{0:T(256)(128)(2,1)S(1)}, bf16[256]{0:T(256)(128)(2,1)S(1)}, u32[]{:S(2)}, u32[]{:S(2)}) %collective-permute-start.18) | collective-permute-done | bytes 544 | tf_op jit(solution)/shard_map/ppermute | solution.py:151
  40.3 1.6 %collective-permute-start.19 = (bf16[512]{0:T(512)(128)(2,1)S(1)}, bf16[512]{0:T(512)(128)(2,1)S(1)}, u32[]{:S(2)}, u32[]{:S(2)}) collective-permute-start(bf16[512]{0:T(512)(128)(2,1)S(1)} %maximum_select_fusion.7), channel_id=1, source_target_pairs={{0,2},{1,3},{2,0},{3,1},{4,6},{5,7},{6,4},{7,5},{8,10},{9,11},{10,... | collective-permute-start | bytes 3080 | tf_op jit(solution)/shard_map/ppermute | solution.py:151
  41.8 2.1 %collective-permute-done.19 = bf16[512]{0:T(512)(128)(2,1)S(1)} collective-permute-done((bf16[512]{0:T(512)(128)(2,1)S(1)}, bf16[512]{0:T(512)(128)(2,1)S(1)}, u32[]{:S(2)}, u32[]{:S(2)}) %collective-permute-start.19) | collective-permute-done | bytes 1056 | tf_op jit(solution)/shard_map/ppermute | solution.py:151
  43.9 3.1 %collective-permute-start.20 = (bf16[1024]{0:T(1024)(128)(2,1)S(1)}, bf16[1024]{0:T(1024)(128)(2,1)S(1)}, u32[]{:S(2)}, u32[]{:S(2)}) collective-permute-start(bf16[1024]{0:T(1024)(128)(2,1)S(1)} %maximum_select_fusion.6), channel_id=1, source_target_pairs={{0,4},{1,5},{2,6},{3,7},{4,0},{5,1},{6,2},{7,3},{8,12},{9,13},{10,... | collective-permute-start | bytes 6152 | tf_op jit(solution)/shard_map/ppermute | solution.py:151
  47.0 2.1 %collective-permute-done.20 = bf16[1024]{0:T(1024)(128)(2,1)S(1)} collective-permute-done((bf16[1024]{0:T(1024)(128)(2,1)S(1)}, bf16[1024]{0:T(1024)(128)(2,1)S(1)}, u32[]{:S(2)}, u32[]{:S(2)}) %collective-permute-start.20) | collective-permute-done | bytes 2080 | tf_op jit(solution)/shard_map/ppermute | solution.py:151
  49.1 1.6 %collective-permute-start.21 = (bf16[2048]{0:T(1024)(128)(2,1)S(1)}, bf16[2048]{0:T(1024)(128)(2,1)S(1)}, u32[]{:S(2)}, u32[]{:S(2)}) collective-permute-start(bf16[2048]{0:T(1024)(128)(2,1)S(1)} %maximum_select_fusion.4), channel_id=1, source_target_pairs={{0,8},{1,33},{2,10},{3,35},{4,12},{5,37},{6,14},{7,39},{8,0},{9,41... | collective-permute-start | bytes 12296 | tf_op jit(solution)/shard_map/ppermute | solution.py:151
  50.7 2.0 %collective-permute-done.21 = bf16[2048]{0:T(1024)(128)(2,1)S(1)} collective-permute-done((bf16[2048]{0:T(1024)(128)(2,1)S(1)}, bf16[2048]{0:T(1024)(128)(2,1)S(1)}, u32[]{:S(2)}, u32[]{:S(2)}) %collective-permute-start.21) | collective-permute-done | bytes 4128 | tf_op jit(solution)/shard_map/ppermute | solution.py:151
  52.7 2.9 %collective-permute-start.22 = (bf16[4096]{0:T(1024)(128)(2,1)S(1)}, bf16[4096]{0:T(1024)(128)(2,1)S(1)}, u32[]{:S(2)}, u32[]{:S(2)}) collective-permute-start(bf16[4096]{0:T(1024)(128)(2,1)S(1)} %maximum_select_fusion.2), channel_id=1, source_target_pairs={{0,16},{1,65},{2,18},{3,67},{4,20},{5,69},{6,22},{7,71},{8,24},{9,... | collective-permute-start | bytes 24584 | tf_op jit(solution)/shard_map/ppermute | solution.py:151
  55.6 3.7 %collective-permute-start.15 = (bf16[1152,512]{1,0:T(8,128)(2,1)}, bf16[1152,512]{1,0:T(8,128)(2,1)S(1)}, u32[]{:S(2)}, u32[]{:S(2)}) collective-permute-start(bf16[1152,512]{1,0:T(8,128)(2,1)} %merge.1.refs_0_), channel_id=1, source_target_pairs={{0,96},{1,25},{2,98},{3,27},{4,100},{5,29},{6,102},{7,31},{8,104},... | collective-permute-start | bytes 3538952 | tf_op jit(solution)/shard_map/ppermute | solution.py:187
  59.3 2.3 %collective-permute-start.3 = (bf16[1152,512]{1,0:T(8,128)(2,1)}, bf16[1152,512]{1,0:T(8,128)(2,1)S(1)}, u32[]{:S(2)}, u32[]{:S(2)}) collective-permute-start(bf16[1152,512]{1,0:T(8,128)(2,1)} %collective-permute-done.refs_0_), channel_id=1, source_target_pairs={{0,96},{1,25},{2,98},{3,27},{4,100},{5,29},{6,102},{7,31},{8,104},... | collective-permute-start | bytes 3538952 | tf_op jit(solution)/shard_map/ppermute | solution.py:187
  61.7 0.4 collective-permute-start.11
  62.1 1.6 %collective-permute-start.1 = (bf16[1152,512]{1,0:T(8,128)(2,1)}, bf16[1152,512]{1,0:T(8,128)(2,1)S(1)}, u32[]{:S(2)}, u32[]{:S(2)}) collective-permute-start(bf16[1152,512]{1,0:T(8,128)(2,1)} %collective-permute-done.refs_0_), channel_id=1, source_target_pairs={{0,32},{1,9},{2,34},{3,11},{4,36},{5,13},{6,38},{7,15},{8,40},{9,1... | collective-permute-start | bytes 3538952 | tf_op jit(solution)/shard_map/ppermute | solution.py:187
  63.7 1.6 %collective-permute-start.7 = (bf16[1152,512]{1,0:T(8,128)(2,1)}, bf16[1152,512]{1,0:T(8,128)(2,1)}, u32[]{:S(2)}, u32[]{:S(2)}) collective-permute-start(bf16[1152,512]{1,0:T(8,128)(2,1)} %collective-permute-done.5.refs_0_), channel_id=1, source_target_pairs={{0,96},{1,25},{2,98},{3,27},{4,100},{5,29},{6,102},{7,31},{8,104},... | collective-permute-start | bytes 3538952 | tf_op jit(solution)/shard_map/ppermute | solution.py:187
  65.3 8.0 %collective-permute-done.15.refs_1_ = bf16[1152,512]{1,0:T(8,128)(2,1)S(1)} collective-permute-done((bf16[1152,512]{1,0:T(8,128)(2,1)}, bf16[1152,512]{1,0:T(8,128)(2,1)S(1)}, u32[]{:S(2)}, u32[]{:S(2)}) %collective-permute-start.15) | collective-permute-done | bytes 1179680 | tf_op jit(solution)/shard_map/ppermute | solution.py:187
  73.4 1.1 copy-done.1
  74.5 0.2 collective-permute-start.14
  74.6 11.4 %collective-permute-done.3.refs_1_ = bf16[1152,512]{1,0:T(8,128)(2,1)S(1)} collective-permute-done((bf16[1152,512]{1,0:T(8,128)(2,1)}, bf16[1152,512]{1,0:T(8,128)(2,1)S(1)}, u32[]{:S(2)}, u32[]{:S(2)}) %collective-permute-start.3) | collective-permute-done | bytes 1179680 | tf_op jit(solution)/shard_map/ppermute | solution.py:187
  86.0 0.2 collective-permute-start.10
  86.2 12.5 %collective-permute-done.11.refs_1_ = bf16[1152,512]{1,0:T(8,128)(2,1)} collective-permute-done((bf16[1152,512]{1,0:T(8,128)(2,1)}, bf16[1152,512]{1,0:T(8,128)(2,1)}, u32[]{:S(2)}, u32[]{:S(2)}) %collective-permute-start.11) | collective-permute-done | bytes 1179680 | tf_op jit(solution)/shard_map/ppermute | solution.py:187
  98.6 3.7 %collective-permute-start.12 = (bf16[1152,512]{1,0:T(8,128)(2,1)}, bf16[1152,512]{1,0:T(8,128)(2,1)}, u32[]{:S(2)}, u32[]{:S(2)}) collective-permute-start(bf16[1152,512]{1,0:T(8,128)(2,1)} %collective-permute-done.11.refs_1_), channel_id=1, source_target_pairs={{0,96},{1,25},{2,98},{3,27},{4,100},{5,29},{6,102},{7,31},{8,104},... | collective-permute-start | bytes 3538952 | tf_op jit(solution)/shard_map/ppermute | solution.py:187
  102.3 8.9 %collective-permute-done.7.refs_1_ = bf16[1152,512]{1,0:T(8,128)(2,1)} collective-permute-done((bf16[1152,512]{1,0:T(8,128)(2,1)}, bf16[1152,512]{1,0:T(8,128)(2,1)}, u32[]{:S(2)}, u32[]{:S(2)}) %collective-permute-start.7) | collective-permute-done | bytes 1179680 | tf_op jit(solution)/shard_map/ppermute | solution.py:187
  111.3 3.7 %collective-permute-start.8 = (bf16[1152,512]{1,0:T(8,128)(2,1)}, bf16[1152,512]{1,0:T(8,128)(2,1)}, u32[]{:S(2)}, u32[]{:S(2)}) collective-permute-start(bf16[1152,512]{1,0:T(8,128)(2,1)} %collective-permute-done.7.refs_1_), channel_id=1, source_target_pairs={{0,96},{1,25},{2,98},{3,27},{4,100},{5,29},{6,102},{7,31},{8,104},... | collective-permute-start | bytes 3538952 | tf_op jit(solution)/shard_map/ppermute | solution.py:187
  115.0 1.3 copy-done
  116.2 1.3 place.9
  117.5 0.0 copy-start.4
  117.7 0.1 collective-permute-start.2
  117.8 3.2 %collective-permute-start.4 = (bf16[576,512]{1,0:T(8,128)(2,1)S(1)}, bf16[576,512]{1,0:T(8,128)(2,1)S(1)}, u32[]{:S(2)}, u32[]{:S(2)}) collective-permute-start(bf16[576,512]{1,0:T(8,128)(2,1)S(1)} %slice.9), channel_id=1, source_target_pairs={{0,96},{1,25},{2,98},{3,27},{4,100},{5,29},{6,102},{7,31},{8,104},... | collective-permute-start | bytes 1769480 | tf_op jit(solution)/shard_map/ppermute | solution.py:187
  121.1 0.6 copy.42
  121.7 2.7 %place.10 = (bf16[1024,8192]{1,0:T(8,128)(2,1)}, bf16[64,8192]{1,0:T(8,128)(2,1)}, bf16[64,8192]{1,0:T(8,128)(2,1)}) custom-call(bf16[1152,512]{1,0:T(8,128)(2,1)} %collective-permute-done.refs_0_, bf16[1152,512]{1,0:T(8,128)(2,1)} %collective-permute-done.9.refs_1_, ...), custom_call_target="tpu_custom_call", output_to_operand_aliasing={{0}: (2, {}), {1}: (3, {}), {2}: (4, {})} | custom-call | flops 1000000 | bytes 4718592 | tf_op jit(solution)/shard_map/place/pallas_call | solution.py:116
  124.4 2.0 %place.11 = (bf16[1024,8192]{1,0:T(8,128)(2,1)}, bf16[64,8192]{1,0:T(8,128)(2,1)}, bf16[64,8192]{1,0:T(8,128)(2,1)}) custom-call(bf16[1152,512]{1,0:T(8,128)(2,1)S(1)} %collective-permute-done.13.refs_0_, bf16[1152,512]{1,0:T(8,128)(2,1)S(1)} %copy-done.2, ...), custom_call_target="tpu_custom_call", output_to_operand_aliasing={{0}: (2, {}), {1}: (3, {}), {2}: (4, {})} | custom-call | flops 1000000 | bytes 4718592 | tf_op jit(solution)/shard_map/place/pallas_call | solution.py:116
  126.4 2.6 %place.12 = (bf16[1024,8192]{1,0:T(8,128)(2,1)}, bf16[64,8192]{1,0:T(8,128)(2,1)}, bf16[64,8192]{1,0:T(8,128)(2,1)}) custom-call(bf16[1152,512]{1,0:T(8,128)(2,1)} %collective-permute-done.5.refs_0_, bf16[1152,512]{1,0:T(8,128)(2,1)S(1)} %collective-permute-done.3.refs_1_, ...), custom_call_target="tpu_custom_call", output_to_operand_aliasing={{0}: (2, {}), {1}: (3, {}), {2}: (4, {})} | custom-call | flops 1000000 | bytes 4718592 | tf_op jit(solution)/shard_map/place/pallas_call | solution.py:116
  129.0 2.6 %place.13 = (bf16[1024,8192]{1,0:T(8,128)(2,1)}, bf16[64,8192]{1,0:T(8,128)(2,1)}, bf16[64,8192]{1,0:T(8,128)(2,1)}) custom-call(bf16[1152,512]{1,0:T(8,128)(2,1)} %collective-permute-done.14.refs_0_, bf16[1152,512]{1,0:T(8,128)(2,1)} %collective-permute-done.11.refs_1_, ...), custom_call_target="tpu_custom_call", output_to_operand_aliasing={{0}: (2, {}), {1}: (3, {}), {2}: (4, {})} | custom-call | flops 1000000 | bytes 4718592 | tf_op jit(solution)/shard_map/place/pallas_call | solution.py:116
  131.6 2.9 %place.14 = (bf16[1024,8192]{1,0:T(8,128)(2,1)}, bf16[64,8192]{1,0:T(8,128)(2,1)}, bf16[64,8192]{1,0:T(8,128)(2,1)}) custom-call(bf16[1152,512]{1,0:T(8,128)(2,1)S(1)} %collective-permute-done.1.refs_0_, bf16[1152,512]{1,0:T(8,128)(2,1)} %collective-permute-done.7.refs_1_, ...), custom_call_target="tpu_custom_call", output_to_operand_aliasing={{0}: (2, {}), {1}: (3, {}), {2}: (4, {})} | custom-call | flops 1000000 | bytes 4718592 | tf_op jit(solution)/shard_map/place/pallas_call | solution.py:116
  134.4 2.6 %place.15 = (bf16[1024,8192]{1,0:T(8,128)(2,1)}, bf16[64,8192]{1,0:T(8,128)(2,1)}, bf16[64,8192]{1,0:T(8,128)(2,1)}) custom-call(bf16[1152,512]{1,0:T(8,128)(2,1)} %collective-permute-done.10.refs_0_, bf16[1152,512]{1,0:T(8,128)(2,1)} %collective-permute-done.12.refs_1_, ...), custom_call_target="tpu_custom_call", output_to_operand_aliasing={{0}: (2, {}), {1}: (3, {}), {2}: (4, {})} | custom-call | flops 1000000 | bytes 4718592 | tf_op jit(solution)/shard_map/place/pallas_call | solution.py:116
  137.0 2.6 %place.16 = (bf16[1024,8192]{1,0:T(8,128)(2,1)}, bf16[64,8192]{1,0:T(8,128)(2,1)}, bf16[64,8192]{1,0:T(8,128)(2,1)}) custom-call(bf16[1152,512]{1,0:T(8,128)(2,1)} %collective-permute-done.6.refs_0_, bf16[1152,512]{1,0:T(8,128)(2,1)} %collective-permute-done.8.refs_1_, ...), custom_call_target="tpu_custom_call", output_to_operand_aliasing={{0}: (2, {}), {1}: (3, {}), {2}: (4, {})} | custom-call | flops 1000000 | bytes 4718592 | tf_op jit(solution)/shard_map/place/pallas_call | solution.py:116
  139.6 3.1 %collective-permute-done.4.refs_1_ = bf16[576,512]{1,0:T(8,128)(2,1)S(1)} collective-permute-done((bf16[576,512]{1,0:T(8,128)(2,1)S(1)}, bf16[576,512]{1,0:T(8,128)(2,1)S(1)}, u32[]{:S(2)}, u32[]{:S(2)}) %collective-permute-start.4) | collective-permute-done | bytes 589856 | tf_op jit(solution)/shard_map/ppermute | solution.py:187
  142.8 1.4 place.17
  (37 shorter events, 0.2 us)
Async XLA Ops:
  0.6 8.8 %copy-start.5 = (f32[64]{0:T(128)S(1)}, f32[64]{0:T(128)}, u32[]{:S(2)}) copy-start(f32[64]{0:T(128)} %param.20) | copy-start | bytes 772
  0.6 8.8 %copy-start.6 = (f32[64]{0:T(128)S(1)}, f32[64]{0:T(128)}, u32[]{:S(2)}) copy-start(f32[64]{0:T(128)} %param.21) | copy-start | bytes 772
  4.1 27.5 %collective-permute-start = (bf16[1152,512]{1,0:T(8,128)(2,1)}, bf16[1152,512]{1,0:T(8,128)(2,1)}, u32[]{:S(2)}, u32[]{:S(2)}) collective-permute-start(bf16[1152,512]{1,0:T(8,128)(2,1)} %merge.1.refs_0_), channel_id=1, source_target_pairs={{0,8},{1,33},{2,10},{3,35},{4,12},{5,37},{6,14},{7,39},{8,16},{9,4... | collective-permute-start | bytes 3538952 | tf_op jit(solution)/shard_map/ppermute | solution.py:184
  5.9 55.8 %collective-permute-start.9 = (bf16[1152,512]{1,0:T(8,128)(2,1)}, bf16[1152,512]{1,0:T(8,128)(2,1)}, u32[]{:S(2)}, u32[]{:S(2)}) collective-permute-start(bf16[1152,512]{1,0:T(8,128)(2,1)} %merge.1.refs_0_), channel_id=1, source_target_pairs={{0,24},{1,97},{2,26},{3,99},{4,28},{5,101},{6,30},{7,103},{8,0},{9... | collective-permute-start | bytes 3538952 | tf_op jit(solution)/shard_map/ppermute | solution.py:184
  7.4 54.6 %collective-permute-start.13 = (bf16[1152,512]{1,0:T(8,128)(2,1)}, bf16[1152,512]{1,0:T(8,128)(2,1)S(1)}, u32[]{:S(2)}, u32[]{:S(2)}) collective-permute-start(bf16[1152,512]{1,0:T(8,128)(2,1)} %merge.1.refs_0_), channel_id=1, source_target_pairs={{0,32},{1,9},{2,34},{3,11},{4,36},{5,13},{6,38},{7,15},{8,40},{9,1... | collective-permute-start | bytes 3538952 | tf_op jit(solution)/shard_map/ppermute | solution.py:187
  9.5 1.2 collective-permute-start.16
  10.8 21.5 %collective-permute-start.17 = (bf16[128]{0:T(256)(128)(2,1)S(1)}, bf16[128]{0:T(256)(128)(2,1)S(1)}, u32[]{:S(2)}, u32[]{:S(2)}) collective-permute-start(bf16[128]{0:T(256)(128)(2,1)S(1)} %broadcast_select_fusion), channel_id=1, source_target_pairs={{0,32},{1,9},{2,34},{3,11},{4,36},{5,13},{6,38},{7,15},{8,40},{9,1... | collective-permute-start | bytes 776 | tf_op jit(solution)/shard_map/ppermute | solution.py:151
  31.7 32.0 %collective-permute-start.5 = (bf16[1152,512]{1,0:T(8,128)(2,1)}, bf16[1152,512]{1,0:T(8,128)(2,1)}, u32[]{:S(2)}, u32[]{:S(2)}) collective-permute-start(bf16[1152,512]{1,0:T(8,128)(2,1)} %collective-permute-done.refs_0_), channel_id=1, source_target_pairs={{0,8},{1,33},{2,10},{3,35},{4,12},{5,37},{6,14},{7,39},{8,16},{9,4... | collective-permute-start | bytes 3538952 | tf_op jit(solution)/shard_map/ppermute | solution.py:184
  32.4 7.9 %collective-permute-start.18 = (bf16[256]{0:T(256)(128)(2,1)S(1)}, bf16[256]{0:T(256)(128)(2,1)S(1)}, u32[]{:S(2)}, u32[]{:S(2)}) collective-permute-start(bf16[256]{0:T(256)(128)(2,1)S(1)} %broadcast_select_fusion.1), channel_id=1, source_target_pairs={{0,64},{1,17},{2,66},{3,19},{4,68},{5,21},{6,70},{7,23},{8,72},{9,... | collective-permute-start | bytes 1544 | tf_op jit(solution)/shard_map/ppermute | solution.py:151
  40.3 3.6 %collective-permute-start.19 = (bf16[512]{0:T(512)(128)(2,1)S(1)}, bf16[512]{0:T(512)(128)(2,1)S(1)}, u32[]{:S(2)}, u32[]{:S(2)}) collective-permute-start(bf16[512]{0:T(512)(128)(2,1)S(1)} %maximum_select_fusion.7), channel_id=1, source_target_pairs={{0,2},{1,3},{2,0},{3,1},{4,6},{5,7},{6,4},{7,5},{8,10},{9,11},{10,... | collective-permute-start | bytes 3080 | tf_op jit(solution)/shard_map/ppermute | solution.py:151
  43.9 5.2 %collective-permute-start.20 = (bf16[1024]{0:T(1024)(128)(2,1)S(1)}, bf16[1024]{0:T(1024)(128)(2,1)S(1)}, u32[]{:S(2)}, u32[]{:S(2)}) collective-permute-start(bf16[1024]{0:T(1024)(128)(2,1)S(1)} %maximum_select_fusion.6), channel_id=1, source_target_pairs={{0,4},{1,5},{2,6},{3,7},{4,0},{5,1},{6,2},{7,3},{8,12},{9,13},{10,... | collective-permute-start | bytes 6152 | tf_op jit(solution)/shard_map/ppermute | solution.py:151
  49.1 3.6 %collective-permute-start.21 = (bf16[2048]{0:T(1024)(128)(2,1)S(1)}, bf16[2048]{0:T(1024)(128)(2,1)S(1)}, u32[]{:S(2)}, u32[]{:S(2)}) collective-permute-start(bf16[2048]{0:T(1024)(128)(2,1)S(1)} %maximum_select_fusion.4), channel_id=1, source_target_pairs={{0,8},{1,33},{2,10},{3,35},{4,12},{5,37},{6,14},{7,39},{8,0},{9,41... | collective-permute-start | bytes 12296 | tf_op jit(solution)/shard_map/ppermute | solution.py:151
  52.7 6.6 %collective-permute-start.22 = (bf16[4096]{0:T(1024)(128)(2,1)S(1)}, bf16[4096]{0:T(1024)(128)(2,1)S(1)}, u32[]{:S(2)}, u32[]{:S(2)}) collective-permute-start(bf16[4096]{0:T(1024)(128)(2,1)S(1)} %maximum_select_fusion.2), channel_id=1, source_target_pairs={{0,16},{1,65},{2,18},{3,67},{4,20},{5,69},{6,22},{7,71},{8,24},{9,... | collective-permute-start | bytes 24584 | tf_op jit(solution)/shard_map/ppermute | solution.py:151
  55.6 17.8 %collective-permute-start.15 = (bf16[1152,512]{1,0:T(8,128)(2,1)}, bf16[1152,512]{1,0:T(8,128)(2,1)S(1)}, u32[]{:S(2)}, u32[]{:S(2)}) collective-permute-start(bf16[1152,512]{1,0:T(8,128)(2,1)} %merge.1.refs_0_), channel_id=1, source_target_pairs={{0,96},{1,25},{2,98},{3,27},{4,100},{5,29},{6,102},{7,31},{8,104},... | collective-permute-start | bytes 3538952 | tf_op jit(solution)/shard_map/ppermute | solution.py:187
  59.3 2.7 %copy-start.3 = (bf16[4096]{0:T(1024)(128)(2,1)}, bf16[4096]{0:T(1024)(128)(2,1)S(1)}, u32[]{:S(2)}) copy-start(bf16[4096]{0:T(1024)(128)(2,1)S(1)} %collective-permute-done.22) | copy-start | bytes 24580
  59.3 26.7 %collective-permute-start.3 = (bf16[1152,512]{1,0:T(8,128)(2,1)}, bf16[1152,512]{1,0:T(8,128)(2,1)S(1)}, u32[]{:S(2)}, u32[]{:S(2)}) collective-permute-start(bf16[1152,512]{1,0:T(8,128)(2,1)} %collective-permute-done.refs_0_), channel_id=1, source_target_pairs={{0,96},{1,25},{2,98},{3,27},{4,100},{5,29},{6,102},{7,31},{8,104},... | collective-permute-start | bytes 3538952 | tf_op jit(solution)/shard_map/ppermute | solution.py:187
  61.7 37.0 %collective-permute-start.11 = (bf16[1152,512]{1,0:T(8,128)(2,1)}, bf16[1152,512]{1,0:T(8,128)(2,1)}, u32[]{:S(2)}, u32[]{:S(2)}) collective-permute-start(bf16[1152,512]{1,0:T(8,128)(2,1)} %collective-permute-done.9.refs_1_), channel_id=1, source_target_pairs={{0,96},{1,25},{2,98},{3,27},{4,100},{5,29},{6,102},{7,31},{8,104},... | collective-permute-start | bytes 3538952 | tf_op jit(solution)/shard_map/ppermute | solution.py:187
  62.1 40.3 %collective-permute-start.1 = (bf16[1152,512]{1,0:T(8,128)(2,1)}, bf16[1152,512]{1,0:T(8,128)(2,1)S(1)}, u32[]{:S(2)}, u32[]{:S(2)}) collective-permute-start(bf16[1152,512]{1,0:T(8,128)(2,1)} %collective-permute-done.refs_0_), channel_id=1, source_target_pairs={{0,32},{1,9},{2,34},{3,11},{4,36},{5,13},{6,38},{7,15},{8,40},{9,1... | collective-permute-start | bytes 3538952 | tf_op jit(solution)/shard_map/ppermute | solution.py:187
  63.7 47.6 %collective-permute-start.7 = (bf16[1152,512]{1,0:T(8,128)(2,1)}, bf16[1152,512]{1,0:T(8,128)(2,1)}, u32[]{:S(2)}, u32[]{:S(2)}) collective-permute-start(bf16[1152,512]{1,0:T(8,128)(2,1)} %collective-permute-done.5.refs_0_), channel_id=1, source_target_pairs={{0,96},{1,25},{2,98},{3,27},{4,100},{5,29},{6,102},{7,31},{8,104},... | collective-permute-start | bytes 3538952 | tf_op jit(solution)/shard_map/ppermute | solution.py:187
  73.4 1.1 copy-start.1
  74.5 43.2 %collective-permute-start.14 = (bf16[1152,512]{1,0:T(8,128)(2,1)S(1)}, bf16[1152,512]{1,0:T(8,128)(2,1)}, u32[]{:S(2)}, u32[]{:S(2)}) collective-permute-start(bf16[1152,512]{1,0:T(8,128)(2,1)S(1)} %collective-permute-done.13.refs_0_), channel_id=1, source_target_pairs={{0,32},{1,9},{2,34},{3,11},{4,36},{5,13},{6,38},{7,15},{8,40},{9,1... | collective-permute-start | bytes 3538952 | tf_op jit(solution)/shard_map/ppermute | solution.py:187
  86.0 31.7 %collective-permute-start.10 = (bf16[1152,512]{1,0:T(8,128)(2,1)}, bf16[1152,512]{1,0:T(8,128)(2,1)}, u32[]{:S(2)}, u32[]{:S(2)}) collective-permute-start(bf16[1152,512]{1,0:T(8,128)(2,1)} %collective-permute-done.9.refs_1_), channel_id=1, source_target_pairs={{0,32},{1,9},{2,34},{3,11},{4,36},{5,13},{6,38},{7,15},{8,40},{9,1... | collective-permute-start | bytes 3538952 | tf_op jit(solution)/shard_map/ppermute | solution.py:187
  98.6 35.8 %collective-permute-start.12 = (bf16[1152,512]{1,0:T(8,128)(2,1)}, bf16[1152,512]{1,0:T(8,128)(2,1)}, u32[]{:S(2)}, u32[]{:S(2)}) collective-permute-start(bf16[1152,512]{1,0:T(8,128)(2,1)} %collective-permute-done.11.refs_1_), channel_id=1, source_target_pairs={{0,96},{1,25},{2,98},{3,27},{4,100},{5,29},{6,102},{7,31},{8,104},... | collective-permute-start | bytes 3538952 | tf_op jit(solution)/shard_map/ppermute | solution.py:187
  102.3 34.7 %collective-permute-start.6 = (bf16[1152,512]{1,0:T(8,128)(2,1)}, bf16[1152,512]{1,0:T(8,128)(2,1)}, u32[]{:S(2)}, u32[]{:S(2)}) collective-permute-start(bf16[1152,512]{1,0:T(8,128)(2,1)} %collective-permute-done.5.refs_0_), channel_id=1, source_target_pairs={{0,32},{1,9},{2,34},{3,11},{4,36},{5,13},{6,38},{7,15},{8,40},{9,1... | collective-permute-start | bytes 3538952 | tf_op jit(solution)/shard_map/ppermute | solution.py:187
  111.3 25.8 %collective-permute-start.8 = (bf16[1152,512]{1,0:T(8,128)(2,1)}, bf16[1152,512]{1,0:T(8,128)(2,1)}, u32[]{:S(2)}, u32[]{:S(2)}) collective-permute-start(bf16[1152,512]{1,0:T(8,128)(2,1)} %collective-permute-done.7.refs_1_), channel_id=1, source_target_pairs={{0,96},{1,25},{2,98},{3,27},{4,100},{5,29},{6,102},{7,31},{8,104},... | collective-permute-start | bytes 3538952 | tf_op jit(solution)/shard_map/ppermute | solution.py:187
  115.0 1.3 copy-start
  117.5 3.5 %copy-start.4 = (bf16[4096]{0:T(1024)(128)(2,1)S(1)}, bf16[4096]{0:T(1024)(128)(2,1)}, u32[]{:S(2)}) copy-start(bf16[4096]{0:T(1024)(128)(2,1)} %copy-done.3) | copy-start | bytes 24580
  117.7 22.0 %collective-permute-start.2 = (bf16[576,512]{1,0:T(8,128)(2,1)S(1)}, bf16[576,512]{1,0:T(8,128)(2,1)S(1)}, u32[]{:S(2)}, u32[]{:S(2)}) collective-permute-start(bf16[576,512]{1,0:T(8,128)(2,1)S(1)} %slice.8), channel_id=1, source_target_pairs={{0,32},{1,9},{2,34},{3,11},{4,36},{5,13},{6,38},{7,15},{8,40},{9,1... | collective-permute-start | bytes 1769480 | tf_op jit(solution)/shard_map/ppermute | solution.py:187
  117.8 25.0 %collective-permute-start.4 = (bf16[576,512]{1,0:T(8,128)(2,1)S(1)}, bf16[576,512]{1,0:T(8,128)(2,1)S(1)}, u32[]{:S(2)}, u32[]{:S(2)}) collective-permute-start(bf16[576,512]{1,0:T(8,128)(2,1)S(1)} %slice.9), channel_id=1, source_target_pairs={{0,96},{1,25},{2,98},{3,27},{4,100},{5,29},{6,102},{7,31},{8,104},... | collective-permute-start | bytes 1769480 | tf_op jit(solution)/shard_map/ppermute | solution.py:187
  121.7 2.7 %copy-start.2 = (bf16[1152,512]{1,0:T(8,128)(2,1)S(1)}, bf16[1152,512]{1,0:T(8,128)(2,1)}, u32[]{:S(2)}) copy-start(bf16[1152,512]{1,0:T(8,128)(2,1)} %copy-done.1) | copy-start | bytes 3538948

commit v2 on v1

v2 whole, which is shorter than its diff:
```python
import functools
import jax
import jax.numpy as jnp
from jax import lax
from jax.experimental import pallas as pl
from jax.experimental.pallas import tpu as pltpu
from jax.sharding import PartitionSpec as P


mix_rate = 1.0


SIDE = 4
CORES = 2
STEP = 128
CHUNK = 256
MERGE_VMEM = 65_000_000
PARTS = 2


def product(left, right):
    return lax.dot_general(right, left, (((0,), (0,)), ((), ())), preferred_element_type=jnp.float32)


def fill(train_copies, parts, train, low, high, out):
    for copy, part in zip(train_copies, parts):
        copy.wait()
        for at in range(0, train.shape[1], CHUNK):
            base = train[part, at : at + CHUNK].T.astype(jnp.float32)
            whole = base + mix_rate * product(low[:, part], high[:, at : at + CHUNK])
            out[at : at + CHUNK, part] = whole.astype(jnp.bfloat16)


def merge_kernel(*refs):
    out, side, held, sem = refs[9], refs[10], refs[11:-1], refs[-1]
    train, low, high, key, low_key, high_key, value, low_value, high_value = held
    rows, wide = train.shape
    parts = [pl.ds(at, STEP) for at in range(0, rows, STEP)]
    rest = len(parts)
    copies = [pltpu.make_async_copy(refs[0].at[part], train.at[part], sem.at[i]) for i, part in enumerate(parts)]
    copies += [pltpu.make_async_copy(refs[i], held[i], sem.at[rest + i - 1]) for i in range(1, 9)]
    order = [rest, rest + 1, *range(rest), *range(rest + 2, rest + 8)]
    for i in order:
        copies[i].start()
    copies[rest].wait()
    copies[rest + 1].wait()
    fill(copies, parts, train, low, high, out)
    for copy in copies[rest + 2 :]:
        copy.wait()
    at = wide
    for base, left, right in ((key, low_key, high_key), (value, low_value, high_value)):
        whole = base[...].astype(jnp.float32) + mix_rate * product(left[...], right[...])
        whole = whole.astype(jnp.bfloat16)
        out[at : at + base.shape[0], :] = whole
        side[at - wide : at - wide + base.shape[0], :] = whole
        at += base.shape[0]
    side[at - wide :, :] = low[...]


def merged(train, low, high, train_key, low_key, high_key, train_value, low_value, high_value):
    rows, columns = train.shape
    extra = train_key.shape[1] + train_value.shape[1]
    small = (low.T, high, train_key.T, low_key.T, high_key, train_value.T, low_value.T, high_value)
    return pl.pallas_call(
        merge_kernel,
        in_specs=[pl.BlockSpec(memory_space=pltpu.HBM)] * 9,
        out_specs=[pl.BlockSpec(memory_space=pltpu.VMEM)] * 2,
        out_shape=[
            jax.ShapeDtypeStruct((columns + extra, rows), jnp.bfloat16),
            jax.ShapeDtypeStruct((extra + low.shape[1], rows), jnp.bfloat16),
        ],
        scratch_shapes=[
            pltpu.VMEM(train.shape, train.dtype),
            *[pltpu.VMEM(x.shape, x.dtype) for x in small],
            pltpu.SemaphoreType.DMA((8 + rows // STEP,)),
        ],
        compiler_params=pltpu.CompilerParams(vmem_limit_bytes=MERGE_VMEM),
        cost_estimate=pl.CostEstimate(flops=10**9, bytes_accessed=1, transcendentals=0),
        name="merge",
    )(train, *small)


def finish_kernel(train_ref, side_ref, high_ref, out, train, side, high, sem):
    rows, wide = train.shape
    extra = out.shape[0] - wide
    parts = [pl.ds(at, STEP) for at in range(0, rows, STEP)]
    rest = len(parts)
    copies = [pltpu.make_async_copy(train_ref.at[part], train.at[part], sem.at[i]) for i, part in enumerate(parts)]
    copies.append(pltpu.make_async_copy(side_ref, side, sem.at[rest]))
    copies.append(pltpu.make_async_copy(high_ref, high, sem.at[rest + 1]))
    for copy in copies[rest:] + copies[:rest]:
        copy.start()
    copies[rest].wait()
    copies[rest + 1].wait()
    out[wide:, :] = side[:extra, :]
    fill(copies, parts, train, side.at[pl.ds(extra, side.shape[0] - extra)], high, out)


def finished(train, side, high):
    rows, wide = train.shape
    extra = side.shape[0] - high.shape[0]
    return pl.pallas_call(
        finish_kernel,
        in_specs=[pl.BlockSpec(memory_space=pl.ANY)] * 3,
        out_specs=pl.BlockSpec(memory_space=pltpu.VMEM),
        out_shape=jax.ShapeDtypeStruct((wide + extra, rows), jnp.bfloat16),
        scratch_shapes=[
            *[pltpu.VMEM(x.shape, x.dtype) for x in (train, side, high)],
            pltpu.SemaphoreType.DMA((2 + rows // STEP,)),
        ],
        compiler_params=pltpu.CompilerParams(vmem_limit_bytes=8 << 20),
        cost_estimate=pl.CostEstimate(flops=10**9, bytes_accessed=1, transcendentals=0),
        name="finish",
    )(train, side, high)


def place_kernel(plan, direct, *refs):
    count = len(plan)
    pieces = refs[:count]
    outs, held, into, out_of = refs[-count - 5 : -count - 2], refs[-count - 2 : -2], refs[-2], refs[-1]
    rank = lax.axis_index("rows")
    first_axis_is_y = lax.rem(lax.axis_index("cols"), CORES) == 0
    y, z = lax.rem(rank, SIDE), lax.div(rank, SIDE)
    reads, writes = [], []
    for piece, kept, straight, (first, one, two) in zip(pieces, held, direct, plan):
        dy, dz = jnp.where(first_axis_is_y, one, two), jnp.where(first_axis_is_y, two, one)
        origin = lax.rem(z + dz, SIDE) * SIDE + lax.rem(y + dy, SIDE)
        width = piece.shape[1]
        at = pl.ds(pl.multiple_of(origin * width, width), width)
        half = piece.shape[0] // PARTS
        for part in range(PARTS):
            low, high = part * half, (part + 1) * half
            if straight:
                kept = piece
                reads.append(None)
            else:
                reads.append(
                    pltpu.make_async_copy(piece.at[pl.ds(low, half)], kept.at[pl.ds(low, half)], into.at[len(reads)])
                )
            group, start = [], 0
            for out in outs:
                stop = start + out.shape[0]
                begin, end = max(start, first + low), min(stop, first + high)
                if begin < end:
                    group.append((kept.at[pl.ds(begin - first, end - begin)], out.at[pl.ds(begin - start, end - begin), at]))
                start = stop
            writes.append(group)
    for read in reads:
        if read is not None:
            read.start()
    started = []
    for read, group in sorted(zip(reads, writes), key=lambda both: both[0] is not None):
        if read is not None:
            read.wait()
        for source, target in group:
            started.append(pltpu.make_async_copy(source, target, out_of.at[len(started)]))
            started[-1].start()
    for copy in started:
        copy.wait()


def place(pieces, plan, outs, shapes, direct):
    count = len(pieces)
    hbm = pl.BlockSpec(memory_space=pltpu.HBM)
    given = () if outs is None else outs
    return pl.pallas_call(
        functools.partial(place_kernel, tuple(plan), direct),
        in_specs=[pl.BlockSpec(memory_space=pl.ANY)] * count + [hbm] * len(given),
        out_specs=[hbm] * 3,
        out_shape=shapes,
        scratch_shapes=[
            *[pltpu.VMEM((16, 128) if straight else p.shape, p.dtype) for p, straight in zip(pieces, direct)],
            pltpu.SemaphoreType.DMA((PARTS * count,)),
            pltpu.SemaphoreType.DMA((PARTS * count + 3 * count,)),
        ],
        input_output_aliases={count + i: i for i in range(len(given))},
        compiler_params=pltpu.CompilerParams(vmem_limit_bytes=5 << 20),
        cost_estimate=pl.CostEstimate(
            flops=10**6, bytes_accessed=4 * sum(p.size for p in pieces), transcendentals=0
        ),
        name="place",
    )(*pieces, *given)


def along(second, by):
    pairs = []
    for z in range(SIDE):
        for y in range(SIDE):
            for x in range(SIDE):
                for core in range(CORES):
                    on_z = (core == 1) != second
                    to_z, to_y = ((z + by) % SIDE, y) if on_z else (z, (y + by) % SIDE)
                    flat = lambda r, q: ((r * SIDE + q) * SIDE + x) * CORES + core
                    pairs.append((flat(z, y), flat(to_z, to_y)))
    return pairs


def join_kernel(mine_ref, other_ref, out_ref):
    rows, width = mine_ref.shape
    out_ref[:rows, :width] = mine_ref[...]
    if out_ref.shape[0] > rows:
        out_ref[rows:, :] = other_ref[...]
    else:
        out_ref[:, width:] = other_ref[...]


def joined(mine, other, wider):
    rows, width = mine.shape
    vmem = pl.BlockSpec(memory_space=pltpu.VMEM)
    return pl.pallas_call(
        join_kernel,
        in_specs=[vmem] * 2,
        out_specs=vmem,
        out_shape=jax.ShapeDtypeStruct((rows, 2 * width) if wider else (2 * rows, width), mine.dtype),
        compiler_params=pltpu.CompilerParams(vmem_limit_bytes=1 << 20),
        name="join",
    )(mine, other)


def exchange(mine, bit, swapped):
    count = SIDE * SIDE * SIDE * CORES
    pick = lambda i: swapped if i % CORES else bit
    other = lax.ppermute(mine, ("rows", "cols"), [(i, i ^ pick(i)) for i in range(count)])
    return joined(mine, other, bit == 1)


def order_kernel(norm_ref, out_ref, rows, held):
    cell, rank = lax.axis_index("cols"), lax.axis_index("rows")
    core, x = lax.rem(cell, CORES), lax.div(cell, CORES)
    y, z = lax.rem(rank, SIDE), lax.div(rank, SIDE)
    side = norm_ref.shape[1] // 2
    rolled = pltpu.roll(norm_ref[...], side, 1)
    held[...] = jnp.where(core == 0, norm_ref[...], rolled)
    for i in range(SIDE * SIDE * SIDE):
        dz, dy, dx = (i // 16) ^ z, (i // 4 % 4) ^ y, (i % 4) ^ x
        row = jnp.where(core == 0, dy * 16 + dx * 4 + dz, dz * 16 + dx * 4 + dy)
        rows[pl.ds(i, 1), :] = held[pl.ds(row, 1), :]
    out_ref[...] = rows[...].astype(jnp.bfloat16)


def in_order(norm):
    vmem = pl.BlockSpec(memory_space=pltpu.VMEM)
    return pl.pallas_call(
        order_kernel,
        in_specs=[vmem],
        out_specs=vmem,
        out_shape=jax.ShapeDtypeStruct(norm.shape, jnp.bfloat16),
        scratch_shapes=[pltpu.VMEM(norm.shape, norm.dtype)] * 2,
        compiler_params=pltpu.CompilerParams(vmem_limit_bytes=1 << 20),
        name="order",
    )(norm).reshape(-1)


def body(
    train_query,
    low_query,
    high_query,
    train_key,
    low_key,
    high_key,
    train_value,
    low_value,
    high_value,
    norm_train,
    norm_step,
):
    shapes = [
        jax.ShapeDtypeStruct((w.shape[1], w.shape[0] * SIDE * SIDE), jnp.bfloat16)
        for w in (train_query, train_key, train_value)
    ]
    own, side = merged(
        train_query, low_query, high_query, train_key, low_key, high_key, train_value, low_value, high_value
    )
    part = own.shape[0] * 13 // 24

    def one(x, by):
        return lax.ppermute(x, ("rows", "cols"), along(False, by))

    def two(x, by):
        return lax.ppermute(x, ("rows", "cols"), along(True, by))

    outs = None

    def put(name, pieces, plan, direct=()):
        nonlocal outs
        direct = (name != "put_own",) * len(pieces)
        outs = place(pieces, plan, outs, shapes, direct)

    raw_up, raw_down = one(train_query, 1), one(train_query, -1)
    side_up, side_down = one(side, 1), one(side, -1)
    a_up = finished(raw_up, side_up, high_query)
    a_down = finished(raw_down, side_down, high_query)
    norm = (norm_train + norm_step).reshape(1, -1)
    norm = exchange(norm, 1, 1)
    norm = exchange(norm, 32, 8)
    norm = exchange(norm, 64, 16)
    c_up, c_down = two(own, 1), two(own, -1)
    b = one(a_up, 1)
    d_down, d_up = two(a_up, -1), two(a_up, 1)
    g_down, g_up = two(a_down, -1), two(a_down, 1)
    far = two(c_down, -1)
    put("put_own", [own], [(0, 0, 0)])
    put("put_c", [c_up, c_down], [(0, 0, 3), (0, 0, 1)])
    put("put_a", [a_up, a_down], [(0, 3, 0), (0, 1, 0)])
    norm = exchange(norm, 2, 2)
    norm = exchange(norm, 4, 4)
    e_down, e_up = two(b, -1), two(b, 1)
    put("put_b", [b, d_down], [(0, 2, 0), (0, 3, 1)])
    norm = exchange(norm, 8, 32)
    d_far_low = two(d_down[part:], -1)
    put("put_d", [d_up, g_down], [(0, 3, 3), (0, 1, 1)])
    norm = exchange(norm, 16, 64)
    g_far = two(g_up, 1)
    d_far_top = two(d_up[:part], 1)
    put("put_g", [g_up, far], [(0, 1, 3), (0, 0, 2)])
    e_far = two(e_down, -1)
    put("put_e", [e_up, e_down], [(0, 2, 3), (0, 2, 1)])
    serve_norm = in_order(norm)
    put("put_f", [g_far, d_far_low], [(0, 1, 2), (part, 3, 2)])
    put("put_h", [e_far, d_far_top], [(0, 2, 2), (0, 3, 2)])
    return (*outs, serve_norm)


def solution(mesh):
    return jax.shard_map(
        body,
        mesh=mesh,
        in_specs=(
            P("rows", "cols"),
            P("rows", None),
            P(None, "cols"),
            P("rows", "cols"),
            P("rows", None),
            P(None, "cols"),
            P("rows", "cols"),
            P("rows", None),
            P(None, "cols"),
            P(("rows", "cols")),
            P(("rows", "cols")),
        ),
        out_specs=(P("cols", None), P("cols", None), P("cols", None), P()),
        check_vma=False,
    )
```

time: 144 us -> 130 us (0.903)
  waiting for transfers between devices: 71.8 us -> 65.7 us
  Pallas kernels: 24 us -> 20.8 us
  local copies, waits for them, and re-layouts: 3.09 us -> 0.1 us
  starting transfers between devices: 44.2 us -> 42.2 us
    ppermute x3 -> x5, waiting for transfers between devices: 18.9 us -> 7.31 us  [one(): return lax.ppermute(x, ('rows', 'cols'), along(False, by))]
    ppermute x7, waiting for transfers between devices: 8.87 us -> 14.5 us  [exchange(): lax.ppermute(mine, ('rows', 'cols'), [(i, i ^ pick(i)) for i in range(cou...]
    ppermute x7, starting transfers between devices: 17.5 us -> 13.5 us  [exchange(): lax.ppermute(mine, ('rows', 'cols'), [(i, i ^ pick(i)) for i in range(cou...]
    ppermute x3 -> x5, starting transfers between devices: 3.98 us -> 7.41 us  [one(): return lax.ppermute(x, ('rows', 'cols'), along(False, by))]
    pallas_call x9 -> x19, Pallas kernels: 20.5 us -> 17.2 us  [the longest x9 13.1 us: place(): pl.pallas_call(functools.partial(place_kernel, tuple(plan), direct), in_s...]
    unnamed x14 -> x12, local copies, waits for them, and re-layouts: 2.4 us -> 0.02 us
    ppermute x13, starting transfers between devices: 22.7 us -> 21.3 us  [two(): return lax.ppermute(x, ('rows', 'cols'), along(True, by))]
  transfers between devices with their start and end apart: 23 -> 25, of which waited for: 11 -> 13; matrix products, arithmetic and copies ran while one was open for 1% -> 0% of each run, Pallas kernels for 13% -> 15%
where the time goes in v2:
time: 130 us
  waiting for transfers between devices  65.7 us (51%)
  starting transfers between devices  42.2 us (32%)
  Pallas kernels  20.8 us (16%)
    ppermute x13, waiting for transfers between devices, two(): return lax.ppermute(x, ('rows', 'cols'), along(True, by))  43.9 us
    ppermute x13, starting transfers between devices, two(): return lax.ppermute(x, ('rows', 'cols'), along(True, by))  21.3 us
    ppermute x7, waiting for transfers between devices, exchange(): lax.ppermute(mine, ('rows', 'cols'), [(i, i ^ pick(i)) for i in range(cou...  14.5 us
    ppermute x7, starting transfers between devices, exchange(): lax.ppermute(mine, ('rows', 'cols'), [(i, i ^ pick(i)) for i in range(cou...  13.5 us
    pallas_call x9, Pallas kernels, place(): pl.pallas_call(functools.partial(place_kernel, tuple(plan), direct), in_s...  13.1 us
    ppermute x5, starting transfers between devices, one(): return lax.ppermute(x, ('rows', 'cols'), along(False, by))  7.41 us
    ppermute x5, waiting for transfers between devices, one(): return lax.ppermute(x, ('rows', 'cols'), along(False, by))  7.31 us
    pallas_call x1, Pallas kernels, merged(): pl.pallas_call(merge_kernel, in_specs=[pl.BlockSpec(memory_space=pltpu.HB...  3.55 us
  transfers between devices with their start and end apart: 25, of which 13 were waited for; matrix products, arithmetic and copies ran while one was open for 0% of the time, Pallas kernels for 15%

profile of v2, /device:TPU:0, one launch (start us, length us, event | category | flops | bytes accessed | tf_op | source)
XLA Modules:
  0.0 129.6 jit_solution(18287504722864105243)
XLA Ops:
  0.6 1.8 %collective-permute-start = (bf16[512,1024]{1,0:T(8,128)(2,1)}, bf16[512,1024]{1,0:T(8,128)(2,1)S(1)}, u32[]{:S(2)}, u32[]{:S(2)}) collective-permute-start(bf16[512,1024]{1,0:T(8,128)(2,1)} %refs_0_.1), channel_id=1, source_target_pairs={{0,8},{1,33},{2,10},{3,35},{4,12},{5,37},{6,14},{7,39},{8,16},{9,4... | collective-permute-start | bytes 3145736 | tf_op jit(solution)/shard_map/ppermute | solution.py:277
  2.4 3.6 %merge.1 = (bf16[1152,512]{1,0:T(8,128)(2,1)}, bf16[192,512]{1,0:T(8,128)(2,1)}) custom-call(bf16[512,1024]{1,0:T(8,128)(2,1)} %refs_0_.1, bf16[64,512]{1,0:T(8,128)(2,1)} %bitcast.9, bf16[64,1024]{1,0:T(8,128)(2,1)} %high_ref.3, bf16[64,512]{1,0:T(8,128)(2,1)} %bitcast.10, bf16[64,512]{1,0:T(8,128)(2,1)} %bitcast.11, bf16[64,64]{1,0:T(8,128)(2,1)} %refs_5_.1, ...), custom_call_target="tpu_custom_call" | custom-call | flops 1000000000 | bytes 1 | tf_op jit(solution)/shard_map/merge/pallas_call | solution.py:64
  6.0 1.6 %collective-permute-start.1 = (bf16[192,512]{1,0:T(8,128)(2,1)}, bf16[192,512]{1,0:T(8,128)(2,1)S(1)}, u32[]{:S(2)}, u32[]{:S(2)}) collective-permute-start(bf16[192,512]{1,0:T(8,128)(2,1)} %get-tuple-element.33), channel_id=1, source_target_pairs={{0,8},{1,33},{2,10},{3,35},{4,12},{5,37},{6,14},{7,39},{8,16},{9,4... | collective-permute-start | bytes 589832 | tf_op jit(solution)/shard_map/ppermute | solution.py:277
  7.6 4.1 %collective-permute-start.14 = (bf16[1152,512]{1,0:T(8,128)(2,1)}, bf16[1152,512]{1,0:T(8,128)(2,1)S(1)}, u32[]{:S(2)}, u32[]{:S(2)}) collective-permute-start(bf16[1152,512]{1,0:T(8,128)(2,1)} %get-tuple-element.34.refs_0_), channel_id=1, source_target_pairs={{0,96},{1,25},{2,98},{3,27},{4,100},{5,29},{6,102},{7,31},{8,104},... | collective-permute-start | bytes 3538952 | tf_op jit(solution)/shard_map/ppermute | solution.py:280
  11.7 7.3 %collective-permute-done.1.side_ref = bf16[192,512]{1,0:T(8,128)(2,1)S(1)} collective-permute-done((bf16[192,512]{1,0:T(8,128)(2,1)}, bf16[192,512]{1,0:T(8,128)(2,1)S(1)}, u32[]{:S(2)}, u32[]{:S(2)}) %collective-permute-start.1) | collective-permute-done | bytes 196640 | tf_op jit(solution)/shard_map/ppermute | solution.py:277
  19.0 1.6 %finish.2.refs_0_ = bf16[1152,512]{1,0:T(8,128)(2,1)S(1)} custom-call(bf16[512,1024]{1,0:T(8,128)(2,1)S(1)} %collective-permute-done.train_ref, bf16[192,512]{1,0:T(8,128)(2,1)S(1)} %collective-permute-done.1.side_ref, bf16[64,1024]{1,0:T(8,128)(2,1)S(1)} %copy-done.1), custom_call_target="tpu_custom_call" | custom-call | flops 1000000000 | bytes 1 | tf_op jit(solution)/shard_map/finish/pallas_call | solution.py:102
  20.7 0.5 collective-permute-start.2
  21.2 2.8 %collective-permute-start.7 = (bf16[512,1024]{1,0:T(8,128)(2,1)S(1)}, bf16[512,1024]{1,0:T(8,128)(2,1)S(1)}, u32[]{:S(2)}, u32[]{:S(2)}) collective-permute-start(bf16[512,1024]{1,0:T(8,128)(2,1)S(1)} %copy-done.2), channel_id=1, source_target_pairs={{0,24},{1,97},{2,26},{3,99},{4,28},{5,101},{6,30},{7,103},{8,0},{9... | collective-permute-start | bytes 3145736 | tf_op jit(solution)/shard_map/ppermute | solution.py:277
  24.0 0.7 collective-permute-start.8
  24.7 0.1 collective-permute-start.18
  24.8 1.1 collective-permute-done.18.other_ref
  26.0 1.9 %collective-permute-start.19 = (f32[1,128]{1,0:T(1,128)S(1)}, f32[1,128]{1,0:T(1,128)S(1)}, u32[]{:S(2)}, u32[]{:S(2)}) collective-permute-start(f32[1,128]{1,0:T(1,128)S(1)} %join.7.mine_ref), channel_id=1, source_target_pairs={{0,32},{1,9},{2,34},{3,11},{4,36},{5,13},{6,38},{7,15},{8,40},{9,1... | collective-permute-start | bytes 1544 | tf_op jit(solution)/shard_map/ppermute | solution.py:223
  27.9 1.7 %collective-permute-done.19.other_ref = f32[1,128]{1,0:T(1,128)S(1)} collective-permute-done((f32[1,128]{1,0:T(1,128)S(1)}, f32[1,128]{1,0:T(1,128)S(1)}, u32[]{:S(2)}, u32[]{:S(2)}) %collective-permute-start.19) | collective-permute-done | bytes 544 | tf_op jit(solution)/shard_map/ppermute | solution.py:223
  29.6 3.9 %collective-permute-start.20 = (f32[2,128]{1,0:T(2,128)S(1)}, f32[2,128]{1,0:T(2,128)S(1)}, u32[]{:S(2)}, u32[]{:S(2)}) collective-permute-start(f32[2,128]{1,0:T(2,128)S(1)} %join.8.mine_ref), channel_id=1, source_target_pairs={{0,64},{1,17},{2,66},{3,19},{4,68},{5,21},{6,70},{7,23},{8,72},{9,... | collective-permute-start | bytes 3080 | tf_op jit(solution)/shard_map/ppermute | solution.py:223
  33.5 1.6 %collective-permute-done.20.other_ref = f32[2,128]{1,0:T(2,128)S(1)} collective-permute-done((f32[2,128]{1,0:T(2,128)S(1)}, f32[2,128]{1,0:T(2,128)S(1)}, u32[]{:S(2)}, u32[]{:S(2)}) %collective-permute-start.20) | collective-permute-done | bytes 1056 | tf_op jit(solution)/shard_map/ppermute | solution.py:223
  35.0 1.5 %collective-permute-start.21 = (f32[4,128]{1,0:T(4,128)S(1)}, f32[4,128]{1,0:T(4,128)S(1)}, u32[]{:S(2)}, u32[]{:S(2)}) collective-permute-start(f32[4,128]{1,0:T(4,128)S(1)} %join.9.mine_ref), channel_id=1, source_target_pairs={{0,2},{1,3},{2,0},{3,1},{4,6},{5,7},{6,4},{7,5},{8,10},{9,11},{10,... | collective-permute-start | bytes 6152 | tf_op jit(solution)/shard_map/ppermute | solution.py:223
  36.5 2.1 %collective-permute-done.21.other_ref = f32[4,128]{1,0:T(4,128)S(1)} collective-permute-done((f32[4,128]{1,0:T(4,128)S(1)}, f32[4,128]{1,0:T(4,128)S(1)}, u32[]{:S(2)}, u32[]{:S(2)}) %collective-permute-start.21) | collective-permute-done | bytes 2080 | tf_op jit(solution)/shard_map/ppermute | solution.py:223
  38.6 3.0 %collective-permute-start.22 = (f32[8,128]{1,0:T(8,128)S(1)}, f32[8,128]{1,0:T(8,128)S(1)}, u32[]{:S(2)}, u32[]{:S(2)}) collective-permute-start(f32[8,128]{1,0:T(8,128)S(1)} %join.10.mine_ref), channel_id=1, source_target_pairs={{0,4},{1,5},{2,6},{3,7},{4,0},{5,1},{6,2},{7,3},{8,12},{9,13},{10,... | collective-permute-start | bytes 12296 | tf_op jit(solution)/shard_map/ppermute | solution.py:223
  41.6 2.1 %collective-permute-done.22.other_ref = f32[8,128]{1,0:T(8,128)S(1)} collective-permute-done((f32[8,128]{1,0:T(8,128)S(1)}, f32[8,128]{1,0:T(8,128)S(1)}, u32[]{:S(2)}, u32[]{:S(2)}) %collective-permute-start.22) | collective-permute-done | bytes 4128 | tf_op jit(solution)/shard_map/ppermute | solution.py:223
  43.7 1.4 %collective-permute-start.23 = (f32[16,128]{1,0:T(8,128)S(1)}, f32[16,128]{1,0:T(8,128)S(1)}, u32[]{:S(2)}, u32[]{:S(2)}) collective-permute-start(f32[16,128]{1,0:T(8,128)S(1)} %join.11.mine_ref), channel_id=1, source_target_pairs={{0,8},{1,33},{2,10},{3,35},{4,12},{5,37},{6,14},{7,39},{8,0},{9,41... | collective-permute-start | bytes 24584 | tf_op jit(solution)/shard_map/ppermute | solution.py:223
  45.2 2.2 %collective-permute-done.23.other_ref = f32[16,128]{1,0:T(8,128)S(1)} collective-permute-done((f32[16,128]{1,0:T(8,128)S(1)}, f32[16,128]{1,0:T(8,128)S(1)}, u32[]{:S(2)}, u32[]{:S(2)}) %collective-permute-start.23) | collective-permute-done | bytes 8224 | tf_op jit(solution)/shard_map/ppermute | solution.py:223
  47.4 1.7 %collective-permute-start.24 = (f32[32,128]{1,0:T(8,128)S(1)}, f32[32,128]{1,0:T(8,128)S(1)}, u32[]{:S(2)}, u32[]{:S(2)}) collective-permute-start(f32[32,128]{1,0:T(8,128)S(1)} %join.12.mine_ref), channel_id=1, source_target_pairs={{0,16},{1,65},{2,18},{3,67},{4,20},{5,69},{6,22},{7,71},{8,24},{9,... | collective-permute-start | bytes 49160 | tf_op jit(solution)/shard_map/ppermute | solution.py:223
  49.0 3.8 %collective-permute-done.24.other_ref = f32[32,128]{1,0:T(8,128)S(1)} collective-permute-done((f32[32,128]{1,0:T(8,128)S(1)}, f32[32,128]{1,0:T(8,128)S(1)}, u32[]{:S(2)}, u32[]{:S(2)}) %collective-permute-start.24) | collective-permute-done | bytes 16416 | tf_op jit(solution)/shard_map/ppermute | solution.py:223
  52.8 1.6 %collective-permute-start.17 = (bf16[1152,512]{1,0:T(8,128)(2,1)S(1)}, bf16[1152,512]{1,0:T(8,128)(2,1)S(1)}, u32[]{:S(2)}, u32[]{:S(2)}) collective-permute-start(bf16[1152,512]{1,0:T(8,128)(2,1)S(1)} %copy-done), channel_id=1, source_target_pairs={{0,32},{1,9},{2,34},{3,11},{4,36},{5,13},{6,38},{7,15},{8,40},{9,1... | collective-permute-start | bytes 3538952 | tf_op jit(solution)/shard_map/ppermute | solution.py:280
  54.4 2.2 %collective-permute-start.11 = (bf16[1152,512]{1,0:T(8,128)(2,1)S(1)}, bf16[1152,512]{1,0:T(8,128)(2,1)S(1)}, u32[]{:S(2)}, u32[]{:S(2)}) collective-permute-start(bf16[1152,512]{1,0:T(8,128)(2,1)S(1)} %finish.2.refs_0_), channel_id=1, source_target_pairs={{0,96},{1,25},{2,98},{3,27},{4,100},{5,29},{6,102},{7,31},{8,104},... | collective-permute-start | bytes 3538952 | tf_op jit(solution)/shard_map/ppermute | solution.py:280
  56.6 1.6 %finish.3.refs_1_ = bf16[1152,512]{1,0:T(8,128)(2,1)S(1)} custom-call(bf16[512,1024]{1,0:T(8,128)(2,1)S(1)} %collective-permute-done.7.train_ref, bf16[192,512]{1,0:T(8,128)(2,1)S(1)} %collective-permute-done.8.side_ref, bf16[64,1024]{1,0:T(8,128)(2,1)S(1)} %copy-done.1), custom_call_target="tpu_custom_call" | custom-call | flops 1000000000 | bytes 1 | tf_op jit(solution)/shard_map/finish/pallas_call | solution.py:102
  58.2 1.8 %collective-permute-start.9 = (bf16[1152,512]{1,0:T(8,128)(2,1)S(1)}, bf16[1152,512]{1,0:T(8,128)(2,1)S(1)}, u32[]{:S(2)}, u32[]{:S(2)}) collective-permute-start(bf16[1152,512]{1,0:T(8,128)(2,1)S(1)} %finish.3.refs_1_), channel_id=1, source_target_pairs={{0,32},{1,9},{2,34},{3,11},{4,36},{5,13},{6,38},{7,15},{8,40},{9,1... | collective-permute-start | bytes 3538952 | tf_op jit(solution)/shard_map/ppermute | solution.py:280
  60.0 1.6 %collective-permute-start.3 = (bf16[1152,512]{1,0:T(8,128)(2,1)S(1)}, bf16[1152,512]{1,0:T(8,128)(2,1)S(1)}, u32[]{:S(2)}, u32[]{:S(2)}) collective-permute-start(bf16[1152,512]{1,0:T(8,128)(2,1)S(1)} %collective-permute-done.2.refs_0_), channel_id=1, source_target_pairs={{0,96},{1,25},{2,98},{3,27},{4,100},{5,29},{6,102},{7,31},{8,104},... | collective-permute-start | bytes 3538952 | tf_op jit(solution)/shard_map/ppermute | solution.py:280
  61.6 9.1 %collective-permute-done.17.refs_0_ = bf16[1152,512]{1,0:T(8,128)(2,1)S(1)} collective-permute-done((bf16[1152,512]{1,0:T(8,128)(2,1)S(1)}, bf16[1152,512]{1,0:T(8,128)(2,1)S(1)}, u32[]{:S(2)}, u32[]{:S(2)}) %collective-permute-start.17) | collective-permute-done | bytes 1179680 | tf_op jit(solution)/shard_map/ppermute | solution.py:280
  70.7 2.0 %collective-permute-start.16 = (bf16[1152,512]{1,0:T(8,128)(2,1)S(1)}, bf16[1152,512]{1,0:T(8,128)(2,1)S(1)}, u32[]{:S(2)}, u32[]{:S(2)}) collective-permute-start(bf16[1152,512]{1,0:T(8,128)(2,1)S(1)} %finish.3.refs_1_), channel_id=1, source_target_pairs={{0,96},{1,25},{2,98},{3,27},{4,100},{5,29},{6,102},{7,31},{8,104},... | collective-permute-start | bytes 3538952 | tf_op jit(solution)/shard_map/ppermute | solution.py:280
  72.7 1.3 collective-permute-start.15
  74.0 9.3 %collective-permute-done.5.refs_0_ = bf16[1152,512]{1,0:T(8,128)(2,1)S(1)} collective-permute-done((bf16[1152,512]{1,0:T(8,128)(2,1)S(1)}, bf16[1152,512]{1,0:T(8,128)(2,1)S(1)}, u32[]{:S(2)}, u32[]{:S(2)}) %collective-permute-start.5) | collective-permute-done | bytes 1179680 | tf_op jit(solution)/shard_map/ppermute | solution.py:280
  83.3 12.6 %collective-permute-done.9.refs_0_ = bf16[1152,512]{1,0:T(8,128)(2,1)S(1)} collective-permute-done((bf16[1152,512]{1,0:T(8,128)(2,1)S(1)}, bf16[1152,512]{1,0:T(8,128)(2,1)S(1)}, u32[]{:S(2)}, u32[]{:S(2)}) %collective-permute-start.9) | collective-permute-done | bytes 1179680 | tf_op jit(solution)/shard_map/ppermute | solution.py:280
  96.0 3.2 %collective-permute-start.4 = (bf16[1152,512]{1,0:T(8,128)(2,1)S(1)}, bf16[1152,512]{1,0:T(8,128)(2,1)S(1)}, u32[]{:S(2)}, u32[]{:S(2)}) collective-permute-start(bf16[1152,512]{1,0:T(8,128)(2,1)S(1)} %collective-permute-done.3.refs_1_), channel_id=1, source_target_pairs={{0,96},{1,25},{2,98},{3,27},{4,100},{5,29},{6,102},{7,31},{8,104},... | collective-permute-start | bytes 3538952 | tf_op jit(solution)/shard_map/ppermute | solution.py:280
  99.3 0.1 collective-permute-start.6
  99.4 9.1 %collective-permute-done.15.refs_1_ = bf16[1152,512]{1,0:T(8,128)(2,1)S(1)} collective-permute-done((bf16[1152,512]{1,0:T(8,128)(2,1)S(1)}, bf16[1152,512]{1,0:T(8,128)(2,1)S(1)}, u32[]{:S(2)}, u32[]{:S(2)}) %collective-permute-start.15) | collective-permute-done | bytes 1179680 | tf_op jit(solution)/shard_map/ppermute | solution.py:280
  108.5 3.4 %collective-permute-start.12 = (bf16[528,512]{1,0:T(8,128)(2,1)S(1)}, bf16[528,512]{1,0:T(8,128)(2,1)S(1)}, u32[]{:S(2)}, u32[]{:S(2)}) collective-permute-start(bf16[528,512]{1,0:T(8,128)(2,1)S(1)} %slice.9), channel_id=1, source_target_pairs={{0,96},{1,25},{2,98},{3,27},{4,100},{5,29},{6,102},{7,31},{8,104},... | collective-permute-start | bytes 1622024 | tf_op jit(solution)/shard_map/ppermute | solution.py:280
  111.9 1.3 place.9
  113.2 0.8 order.1
  114.0 1.5 %place.10 = (bf16[1024,8192]{1,0:T(8,128)(2,1)}, bf16[64,8192]{1,0:T(8,128)(2,1)}, bf16[64,8192]{1,0:T(8,128)(2,1)}) custom-call(bf16[1152,512]{1,0:T(8,128)(2,1)S(1)} %collective-permute-done.17.refs_0_, bf16[1152,512]{1,0:T(8,128)(2,1)S(1)} %collective-permute-done.14.refs_1_, ...), custom_call_target="tpu_custom_call", output_to_operand_aliasing={{0}: (2, {}), {1}: (3, {}), {2}: (4, {})} | custom-call | flops 1000000 | bytes 4718592 | tf_op jit(solution)/shard_map/place/pallas_call | solution.py:166
  115.5 1.5 %place.11 = (bf16[1024,8192]{1,0:T(8,128)(2,1)}, bf16[64,8192]{1,0:T(8,128)(2,1)}, bf16[64,8192]{1,0:T(8,128)(2,1)}) custom-call(bf16[1152,512]{1,0:T(8,128)(2,1)S(1)} %finish.2.refs_0_, bf16[1152,512]{1,0:T(8,128)(2,1)S(1)} %finish.3.refs_1_, ...), custom_call_target="tpu_custom_call", output_to_operand_aliasing={{0}: (2, {}), {1}: (3, {}), {2}: (4, {})} | custom-call | flops 1000000 | bytes 4718592 | tf_op jit(solution)/shard_map/place/pallas_call | solution.py:166
  117.0 1.5 %place.12 = (bf16[1024,8192]{1,0:T(8,128)(2,1)}, bf16[64,8192]{1,0:T(8,128)(2,1)}, bf16[64,8192]{1,0:T(8,128)(2,1)}) custom-call(bf16[1152,512]{1,0:T(8,128)(2,1)S(1)} %collective-permute-done.2.refs_0_, bf16[1152,512]{1,0:T(8,128)(2,1)S(1)} %collective-permute-done.11.refs_1_, ...), custom_call_target="tpu_custom_call", output_to_operand_aliasing={{0}: (2, {}), {1}: (3, {}), {2}: (4, {})} | custom-call | flops 1000000 | bytes 4718592 | tf_op jit(solution)/shard_map/place/pallas_call | solution.py:166
  118.6 1.5 %place.13 = (bf16[1024,8192]{1,0:T(8,128)(2,1)}, bf16[64,8192]{1,0:T(8,128)(2,1)}, bf16[64,8192]{1,0:T(8,128)(2,1)}) custom-call(bf16[1152,512]{1,0:T(8,128)(2,1)S(1)} %collective-permute-done.5.refs_0_, bf16[1152,512]{1,0:T(8,128)(2,1)S(1)} %collective-permute-done.16.refs_1_, ...), custom_call_target="tpu_custom_call", output_to_operand_aliasing={{0}: (2, {}), {1}: (3, {}), {2}: (4, {})} | custom-call | flops 1000000 | bytes 4718592 | tf_op jit(solution)/shard_map/place/pallas_call | solution.py:166
  120.1 1.5 %place.14 = (bf16[1024,8192]{1,0:T(8,128)(2,1)}, bf16[64,8192]{1,0:T(8,128)(2,1)}, bf16[64,8192]{1,0:T(8,128)(2,1)}) custom-call(bf16[1152,512]{1,0:T(8,128)(2,1)S(1)} %collective-permute-done.9.refs_0_, bf16[1152,512]{1,0:T(8,128)(2,1)S(1)} %collective-permute-done.15.refs_1_, ...), custom_call_target="tpu_custom_call", output_to_operand_aliasing={{0}: (2, {}), {1}: (3, {}), {2}: (4, {})} | custom-call | flops 1000000 | bytes 4718592 | tf_op jit(solution)/shard_map/place/pallas_call | solution.py:166
  121.7 1.5 %place.15 = (bf16[1024,8192]{1,0:T(8,128)(2,1)}, bf16[64,8192]{1,0:T(8,128)(2,1)}, bf16[64,8192]{1,0:T(8,128)(2,1)}) custom-call(bf16[1152,512]{1,0:T(8,128)(2,1)S(1)} %collective-permute-done.13.refs_0_, bf16[1152,512]{1,0:T(8,128)(2,1)S(1)} %collective-permute-done.3.refs_1_, ...), custom_call_target="tpu_custom_call", output_to_operand_aliasing={{0}: (2, {}), {1}: (3, {}), {2}: (4, {})} | custom-call | flops 1000000 | bytes 4718592 | tf_op jit(solution)/shard_map/place/pallas_call | solution.py:166
  123.2 3.7 %collective-permute-done.12.refs_1_ = bf16[528,512]{1,0:T(8,128)(2,1)S(1)} collective-permute-done((bf16[528,512]{1,0:T(8,128)(2,1)S(1)}, bf16[528,512]{1,0:T(8,128)(2,1)S(1)}, u32[]{:S(2)}, u32[]{:S(2)}) %collective-permute-start.12) | collective-permute-done | bytes 540704 | tf_op jit(solution)/shard_map/ppermute | solution.py:280
  126.9 1.3 place.16
  128.3 1.4 %place.17 = (bf16[1024,8192]{1,0:T(8,128)(2,1)}, bf16[64,8192]{1,0:T(8,128)(2,1)}, bf16[64,8192]{1,0:T(8,128)(2,1)}) custom-call(bf16[1152,512]{1,0:T(8,128)(2,1)S(1)} %collective-permute-done.4.refs_0_, bf16[624,512]{1,0:T(8,128)(2,1)S(1)} %collective-permute-done.6.refs_1_, ...), custom_call_target="tpu_custom_call", output_to_operand_aliasing={{0}: (2, {}), {1}: (3, {}), {2}: (4, {})} | custom-call | flops 1000000 | bytes 3637248 | tf_op jit(solution)/shard_map/place/pallas_call | solution.py:166
  (37 shorter events, 0.2 us)
Async XLA Ops:
  0.6 18.4 %collective-permute-start = (bf16[512,1024]{1,0:T(8,128)(2,1)}, bf16[512,1024]{1,0:T(8,128)(2,1)S(1)}, u32[]{:S(2)}, u32[]{:S(2)}) collective-permute-start(bf16[512,1024]{1,0:T(8,128)(2,1)} %refs_0_.1), channel_id=1, source_target_pairs={{0,8},{1,33},{2,10},{3,35},{4,12},{5,37},{6,14},{7,39},{8,16},{9,4... | collective-permute-start | bytes 3145736 | tf_op jit(solution)/shard_map/ppermute | solution.py:277
  2.4 16.6 %copy-start.1 = (bf16[64,1024]{1,0:T(8,128)(2,1)S(1)}, bf16[64,1024]{1,0:T(8,128)(2,1)}, u32[]{:S(2)}) copy-start(bf16[64,1024]{1,0:T(8,128)(2,1)} %high_ref.3) | copy-start | bytes 393220
  6.0 13.1 %collective-permute-start.1 = (bf16[192,512]{1,0:T(8,128)(2,1)}, bf16[192,512]{1,0:T(8,128)(2,1)S(1)}, u32[]{:S(2)}, u32[]{:S(2)}) collective-permute-start(bf16[192,512]{1,0:T(8,128)(2,1)} %get-tuple-element.33), channel_id=1, source_target_pairs={{0,8},{1,33},{2,10},{3,35},{4,12},{5,37},{6,14},{7,39},{8,16},{9,4... | collective-permute-start | bytes 589832 | tf_op jit(solution)/shard_map/ppermute | solution.py:277
  7.6 13.6 %copy-start.2 = (bf16[512,1024]{1,0:T(8,128)(2,1)S(1)}, bf16[512,1024]{1,0:T(8,128)(2,1)}, u32[]{:S(2)}) copy-start(bf16[512,1024]{1,0:T(8,128)(2,1)} %refs_0_.1) | copy-start | bytes 3145732
  7.6 16.4 %copy-start.3 = (bf16[192,512]{1,0:T(8,128)(2,1)S(1)}, bf16[192,512]{1,0:T(8,128)(2,1)}, u32[]{:S(2)}) copy-start(bf16[192,512]{1,0:T(8,128)(2,1)} %get-tuple-element.33) | copy-start | bytes 589828
  7.6 17.1 %copy-start.4 = (f32[64]{0:T(128)S(1)}, f32[64]{0:T(128)}, u32[]{:S(2)}) copy-start(f32[64]{0:T(128)} %param.20) | copy-start | bytes 772
  7.6 17.1 %copy-start.5 = (f32[64]{0:T(128)S(1)}, f32[64]{0:T(128)}, u32[]{:S(2)}) copy-start(f32[64]{0:T(128)} %param.21) | copy-start | bytes 772
  7.6 45.2 %copy-start = (bf16[1152,512]{1,0:T(8,128)(2,1)S(1)}, bf16[1152,512]{1,0:T(8,128)(2,1)}, u32[]{:S(2)}) copy-start(bf16[1152,512]{1,0:T(8,128)(2,1)} %get-tuple-element.34.refs_0_) | copy-start | bytes 3538948
  7.6 50.6 %collective-permute-start.14 = (bf16[1152,512]{1,0:T(8,128)(2,1)}, bf16[1152,512]{1,0:T(8,128)(2,1)S(1)}, u32[]{:S(2)}, u32[]{:S(2)}) collective-permute-start(bf16[1152,512]{1,0:T(8,128)(2,1)} %get-tuple-element.34.refs_0_), channel_id=1, source_target_pairs={{0,96},{1,25},{2,98},{3,27},{4,100},{5,29},{6,102},{7,31},{8,104},... | collective-permute-start | bytes 3538952 | tf_op jit(solution)/shard_map/ppermute | solution.py:280
  20.7 39.3 %collective-permute-start.2 = (bf16[1152,512]{1,0:T(8,128)(2,1)S(1)}, bf16[1152,512]{1,0:T(8,128)(2,1)S(1)}, u32[]{:S(2)}, u32[]{:S(2)}) collective-permute-start(bf16[1152,512]{1,0:T(8,128)(2,1)S(1)} %finish.2.refs_0_), channel_id=1, source_target_pairs={{0,8},{1,33},{2,10},{3,35},{4,12},{5,37},{6,14},{7,39},{8,16},{9,4... | collective-permute-start | bytes 3538952 | tf_op jit(solution)/shard_map/ppermute | solution.py:277
  21.2 35.4 %collective-permute-start.7 = (bf16[512,1024]{1,0:T(8,128)(2,1)S(1)}, bf16[512,1024]{1,0:T(8,128)(2,1)S(1)}, u32[]{:S(2)}, u32[]{:S(2)}) collective-permute-start(bf16[512,1024]{1,0:T(8,128)(2,1)S(1)} %copy-done.2), channel_id=1, source_target_pairs={{0,24},{1,97},{2,26},{3,99},{4,28},{5,101},{6,30},{7,103},{8,0},{9... | collective-permute-start | bytes 3145736 | tf_op jit(solution)/shard_map/ppermute | solution.py:277
  24.0 30.4 %collective-permute-start.8 = (bf16[192,512]{1,0:T(8,128)(2,1)S(1)}, bf16[192,512]{1,0:T(8,128)(2,1)S(1)}, u32[]{:S(2)}, u32[]{:S(2)}) collective-permute-start(bf16[192,512]{1,0:T(8,128)(2,1)S(1)} %copy-done.3), channel_id=1, source_target_pairs={{0,24},{1,97},{2,26},{3,99},{4,28},{5,101},{6,30},{7,103},{8,0},{9... | collective-permute-start | bytes 589832 | tf_op jit(solution)/shard_map/ppermute | solution.py:277
  24.7 1.2 collective-permute-start.18
  26.0 3.6 %collective-permute-start.19 = (f32[1,128]{1,0:T(1,128)S(1)}, f32[1,128]{1,0:T(1,128)S(1)}, u32[]{:S(2)}, u32[]{:S(2)}) collective-permute-start(f32[1,128]{1,0:T(1,128)S(1)} %join.7.mine_ref), channel_id=1, source_target_pairs={{0,32},{1,9},{2,34},{3,11},{4,36},{5,13},{6,38},{7,15},{8,40},{9,1... | collective-permute-start | bytes 1544 | tf_op jit(solution)/shard_map/ppermute | solution.py:223
  29.6 5.4 %collective-permute-start.20 = (f32[2,128]{1,0:T(2,128)S(1)}, f32[2,128]{1,0:T(2,128)S(1)}, u32[]{:S(2)}, u32[]{:S(2)}) collective-permute-start(f32[2,128]{1,0:T(2,128)S(1)} %join.8.mine_ref), channel_id=1, source_target_pairs={{0,64},{1,17},{2,66},{3,19},{4,68},{5,21},{6,70},{7,23},{8,72},{9,... | collective-permute-start | bytes 3080 | tf_op jit(solution)/shard_map/ppermute | solution.py:223
  35.0 3.6 %collective-permute-start.21 = (f32[4,128]{1,0:T(4,128)S(1)}, f32[4,128]{1,0:T(4,128)S(1)}, u32[]{:S(2)}, u32[]{:S(2)}) collective-permute-start(f32[4,128]{1,0:T(4,128)S(1)} %join.9.mine_ref), channel_id=1, source_target_pairs={{0,2},{1,3},{2,0},{3,1},{4,6},{5,7},{6,4},{7,5},{8,10},{9,11},{10,... | collective-permute-start | bytes 6152 | tf_op jit(solution)/shard_map/ppermute | solution.py:223
  38.6 5.1 %collective-permute-start.22 = (f32[8,128]{1,0:T(8,128)S(1)}, f32[8,128]{1,0:T(8,128)S(1)}, u32[]{:S(2)}, u32[]{:S(2)}) collective-permute-start(f32[8,128]{1,0:T(8,128)S(1)} %join.10.mine_ref), channel_id=1, source_target_pairs={{0,4},{1,5},{2,6},{3,7},{4,0},{5,1},{6,2},{7,3},{8,12},{9,13},{10,... | collective-permute-start | bytes 12296 | tf_op jit(solution)/shard_map/ppermute | solution.py:223
  43.7 3.7 %collective-permute-start.23 = (f32[16,128]{1,0:T(8,128)S(1)}, f32[16,128]{1,0:T(8,128)S(1)}, u32[]{:S(2)}, u32[]{:S(2)}) collective-permute-start(f32[16,128]{1,0:T(8,128)S(1)} %join.11.mine_ref), channel_id=1, source_target_pairs={{0,8},{1,33},{2,10},{3,35},{4,12},{5,37},{6,14},{7,39},{8,0},{9,41... | collective-permute-start | bytes 24584 | tf_op jit(solution)/shard_map/ppermute | solution.py:223
  47.4 5.4 %collective-permute-start.24 = (f32[32,128]{1,0:T(8,128)S(1)}, f32[32,128]{1,0:T(8,128)S(1)}, u32[]{:S(2)}, u32[]{:S(2)}) collective-permute-start(f32[32,128]{1,0:T(8,128)S(1)} %join.12.mine_ref), channel_id=1, source_target_pairs={{0,16},{1,65},{2,18},{3,67},{4,20},{5,69},{6,22},{7,71},{8,24},{9,... | collective-permute-start | bytes 49160 | tf_op jit(solution)/shard_map/ppermute | solution.py:223
  52.8 17.9 %collective-permute-start.17 = (bf16[1152,512]{1,0:T(8,128)(2,1)S(1)}, bf16[1152,512]{1,0:T(8,128)(2,1)S(1)}, u32[]{:S(2)}, u32[]{:S(2)}) collective-permute-start(bf16[1152,512]{1,0:T(8,128)(2,1)S(1)} %copy-done), channel_id=1, source_target_pairs={{0,32},{1,9},{2,34},{3,11},{4,36},{5,13},{6,38},{7,15},{8,40},{9,1... | collective-permute-start | bytes 3538952 | tf_op jit(solution)/shard_map/ppermute | solution.py:280
  54.4 18.3 %collective-permute-start.11 = (bf16[1152,512]{1,0:T(8,128)(2,1)S(1)}, bf16[1152,512]{1,0:T(8,128)(2,1)S(1)}, u32[]{:S(2)}, u32[]{:S(2)}) collective-permute-start(bf16[1152,512]{1,0:T(8,128)(2,1)S(1)} %finish.2.refs_0_), channel_id=1, source_target_pairs={{0,96},{1,25},{2,98},{3,27},{4,100},{5,29},{6,102},{7,31},{8,104},... | collective-permute-start | bytes 3538952 | tf_op jit(solution)/shard_map/ppermute | solution.py:280
  56.6 26.7 %collective-permute-start.5 = (bf16[1152,512]{1,0:T(8,128)(2,1)S(1)}, bf16[1152,512]{1,0:T(8,128)(2,1)S(1)}, u32[]{:S(2)}, u32[]{:S(2)}) collective-permute-start(bf16[1152,512]{1,0:T(8,128)(2,1)S(1)} %finish.2.refs_0_), channel_id=1, source_target_pairs={{0,32},{1,9},{2,34},{3,11},{4,36},{5,13},{6,38},{7,15},{8,40},{9,1... | collective-permute-start | bytes 3538952 | tf_op jit(solution)/shard_map/ppermute | solution.py:280
  58.2 37.7 %collective-permute-start.9 = (bf16[1152,512]{1,0:T(8,128)(2,1)S(1)}, bf16[1152,512]{1,0:T(8,128)(2,1)S(1)}, u32[]{:S(2)}, u32[]{:S(2)}) collective-permute-start(bf16[1152,512]{1,0:T(8,128)(2,1)S(1)} %finish.3.refs_1_), channel_id=1, source_target_pairs={{0,32},{1,9},{2,34},{3,11},{4,36},{5,13},{6,38},{7,15},{8,40},{9,1... | collective-permute-start | bytes 3538952 | tf_op jit(solution)/shard_map/ppermute | solution.py:280
  60.0 36.0 %collective-permute-start.3 = (bf16[1152,512]{1,0:T(8,128)(2,1)S(1)}, bf16[1152,512]{1,0:T(8,128)(2,1)S(1)}, u32[]{:S(2)}, u32[]{:S(2)}) collective-permute-start(bf16[1152,512]{1,0:T(8,128)(2,1)S(1)} %collective-permute-done.2.refs_0_), channel_id=1, source_target_pairs={{0,96},{1,25},{2,98},{3,27},{4,100},{5,29},{6,102},{7,31},{8,104},... | collective-permute-start | bytes 3538952 | tf_op jit(solution)/shard_map/ppermute | solution.py:280
  70.7 28.6 %collective-permute-start.16 = (bf16[1152,512]{1,0:T(8,128)(2,1)S(1)}, bf16[1152,512]{1,0:T(8,128)(2,1)S(1)}, u32[]{:S(2)}, u32[]{:S(2)}) collective-permute-start(bf16[1152,512]{1,0:T(8,128)(2,1)S(1)} %finish.3.refs_1_), channel_id=1, source_target_pairs={{0,96},{1,25},{2,98},{3,27},{4,100},{5,29},{6,102},{7,31},{8,104},... | collective-permute-start | bytes 3538952 | tf_op jit(solution)/shard_map/ppermute | solution.py:280
  72.7 35.8 %collective-permute-start.15 = (bf16[1152,512]{1,0:T(8,128)(2,1)S(1)}, bf16[1152,512]{1,0:T(8,128)(2,1)S(1)}, u32[]{:S(2)}, u32[]{:S(2)}) collective-permute-start(bf16[1152,512]{1,0:T(8,128)(2,1)S(1)} %collective-permute-done.14.refs_1_), channel_id=1, source_target_pairs={{0,96},{1,25},{2,98},{3,27},{4,100},{5,29},{6,102},{7,31},{8,104},... | collective-permute-start | bytes 3538952 | tf_op jit(solution)/shard_map/ppermute | solution.py:280
  83.3 38.3 %collective-permute-start.13 = (bf16[1152,512]{1,0:T(8,128)(2,1)S(1)}, bf16[1152,512]{1,0:T(8,128)(2,1)S(1)}, u32[]{:S(2)}, u32[]{:S(2)}) collective-permute-start(bf16[1152,512]{1,0:T(8,128)(2,1)S(1)} %collective-permute-done.2.refs_0_), channel_id=1, source_target_pairs={{0,32},{1,9},{2,34},{3,11},{4,36},{5,13},{6,38},{7,15},{8,40},{9,1... | collective-permute-start | bytes 3538952 | tf_op jit(solution)/shard_map/ppermute | solution.py:280
  96.0 31.0 %collective-permute-start.10 = (bf16[1152,512]{1,0:T(8,128)(2,1)S(1)}, bf16[1152,512]{1,0:T(8,128)(2,1)S(1)}, u32[]{:S(2)}, u32[]{:S(2)}) collective-permute-start(bf16[1152,512]{1,0:T(8,128)(2,1)S(1)} %collective-permute-done.9.refs_0_), channel_id=1, source_target_pairs={{0,32},{1,9},{2,34},{3,11},{4,36},{5,13},{6,38},{7,15},{8,40},{9,1... | collective-permute-start | bytes 3538952 | tf_op jit(solution)/shard_map/ppermute | solution.py:280
  96.0 32.3 %collective-permute-start.4 = (bf16[1152,512]{1,0:T(8,128)(2,1)S(1)}, bf16[1152,512]{1,0:T(8,128)(2,1)S(1)}, u32[]{:S(2)}, u32[]{:S(2)}) collective-permute-start(bf16[1152,512]{1,0:T(8,128)(2,1)S(1)} %collective-permute-done.3.refs_1_), channel_id=1, source_target_pairs={{0,96},{1,25},{2,98},{3,27},{4,100},{5,29},{6,102},{7,31},{8,104},... | collective-permute-start | bytes 3538952 | tf_op jit(solution)/shard_map/ppermute | solution.py:280
  99.3 29.0 %collective-permute-start.6 = (bf16[624,512]{1,0:T(8,128)(2,1)S(1)}, bf16[624,512]{1,0:T(8,128)(2,1)S(1)}, u32[]{:S(2)}, u32[]{:S(2)}) collective-permute-start(bf16[624,512]{1,0:T(8,128)(2,1)S(1)} %slice.8), channel_id=1, source_target_pairs={{0,32},{1,9},{2,34},{3,11},{4,36},{5,13},{6,38},{7,15},{8,40},{9,1... | collective-permute-start | bytes 1916936 | tf_op jit(solution)/shard_map/ppermute | solution.py:280
  108.5 18.4 %collective-permute-start.12 = (bf16[528,512]{1,0:T(8,128)(2,1)S(1)}, bf16[528,512]{1,0:T(8,128)(2,1)S(1)}, u32[]{:S(2)}, u32[]{:S(2)}) collective-permute-start(bf16[528,512]{1,0:T(8,128)(2,1)S(1)} %slice.9), channel_id=1, source_target_pairs={{0,96},{1,25},{2,98},{3,27},{4,100},{5,29},{6,102},{7,31},{8,104},... | collective-permute-start | bytes 1622024 | tf_op jit(solution)/shard_map/ppermute | solution.py:280

commit v3 on v2

--- a/solution.py
+++ b/solution.py
@@ -15,7 +15,7 @@
 STEP = 128
 CHUNK = 256
 MERGE_VMEM = 65_000_000
-PARTS = 2
+PARTS = 1
 
 
 def product(left, right):
@@ -271,7 +271,8 @@
     own, side = merged(
         train_query, low_query, high_query, train_key, low_key, high_key, train_value, low_value, high_value
     )
-    part = own.shape[0] * 13 // 24
+    total = own.shape[0]
+    cuts = (total * 5 // 12, total * 19 // 36, train_query.shape[1])
 
     def one(x, by):
         return lax.ppermute(x, ("rows", "cols"), along(False, by))
@@ -303,21 +304,24 @@
     put("put_c", [c_up, c_down], [(0, 0, 3), (0, 0, 1)])
     put("put_a", [a_up, a_down], [(0, 3, 0), (0, 1, 0)])
     norm = exchange(norm, 2, 2)
-    norm = exchange(norm, 4, 4)
+    low1 = two(d_down[cuts[1] : cuts[2]], -1)
+    low2 = two(d_down[cuts[2] :], -1)
     e_down, e_up = two(b, -1), two(b, 1)
     put("put_b", [b, d_down], [(0, 2, 0), (0, 3, 1)])
+    norm = exchange(norm, 4, 4)
+    put("put_d", [d_up, g_down], [(0, 3, 3), (0, 1, 1)])
     norm = exchange(norm, 8, 32)
-    d_far_low = two(d_down[part:], -1)
-    put("put_d", [d_up, g_down], [(0, 3, 3), (0, 1, 1)])
+    g_far = two(g_up, 1)
+    top1 = two(d_up[: cuts[0]], 1)
+    top2 = two(d_up[cuts[0] : cuts[1]], 1)
+    put("put_g", [g_up, low1], [(0, 1, 3), (cuts[1], 3, 2)])
+    e_far = two(e_down, -1)
     norm = exchange(norm, 16, 64)
-    g_far = two(g_up, 1)
-    d_far_top = two(d_up[:part], 1)
-    put("put_g", [g_up, far], [(0, 1, 3), (0, 0, 2)])
-    e_far = two(e_down, -1)
     put("put_e", [e_up, e_down], [(0, 2, 3), (0, 2, 1)])
     serve_norm = in_order(norm)
-    put("put_f", [g_far, d_far_low], [(0, 1, 2), (part, 3, 2)])
-    put("put_h", [e_far, d_far_top], [(0, 2, 2), (0, 3, 2)])
+    put("put_f", [far, g_far], [(0, 0, 2), (0, 1, 2)])
+    put("put_h", [e_far, top1], [(0, 2, 2), (0, 3, 2)])
+    put("put_last", [low2, top2], [(cuts[2], 3, 2), (cuts[0], 3, 2)])
     return (*outs, serve_norm)
 
 

time: 130 us -> 144 us (1.11)
  waiting for transfers between devices: 65.7 us -> 76.5 us
  starting transfers between devices: 42.2 us -> 44.9 us
    ppermute x13 -> x15, waiting for transfers between devices: 43.9 us -> 54.7 us  [two(): return lax.ppermute(x, ('rows', 'cols'), along(True, by))]
    ppermute x13 -> x15, starting transfers between devices: 21.3 us -> 24 us  [two(): return lax.ppermute(x, ('rows', 'cols'), along(True, by))]
    pallas_call x9 -> x10, Pallas kernels: 13.1 us -> 13.6 us  [place(): pl.pallas_call(functools.partial(place_kernel, tuple(plan), direct), in_s...]
  transfers between devices with their start and end apart: 25 -> 27, of which waited for: 13 -> 13; matrix products, arithmetic and copies ran while one was open for 0% -> 0% of each run, Pallas kernels for 15% -> 14%
where the time goes in v3:
time: 144 us
  waiting for transfers between devices  76.5 us (53%)
  starting transfers between devices  44.9 us (31%)
  Pallas kernels  21.2 us (15%)
    ppermute x15, waiting for transfers between devices, two(): return lax.ppermute(x, ('rows', 'cols'), along(True, by))  54.7 us
    ppermute x15, starting transfers between devices, two(): return lax.ppermute(x, ('rows', 'cols'), along(True, by))  24 us
    ppermute x7, waiting for transfers between devices, exchange(): lax.ppermute(mine, ('rows', 'cols'), [(i, i ^ pick(i)) for i in range(cou...  14.5 us
    pallas_call x10, Pallas kernels, place(): pl.pallas_call(functools.partial(place_kernel, tuple(plan), direct), in_s...  13.6 us
    ppermute x7, starting transfers between devices, exchange(): lax.ppermute(mine, ('rows', 'cols'), [(i, i ^ pick(i)) for i in range(cou...  13.5 us
    ppermute x5, starting transfers between devices, one(): return lax.ppermute(x, ('rows', 'cols'), along(False, by))  7.41 us
    ppermute x5, waiting for transfers between devices, one(): return lax.ppermute(x, ('rows', 'cols'), along(False, by))  7.31 us
    pallas_call x1, Pallas kernels, merged(): pl.pallas_call(merge_kernel, in_specs=[pl.BlockSpec(memory_space=pltpu.HB...  3.55 us
  transfers between devices with their start and end apart: 27, of which 13 were waited for; matrix products, arithmetic and copies ran while one was open for 0% of the time, Pallas kernels for 14%

profile of v3, /device:TPU:0, one launch (start us, length us, event | category | flops | bytes accessed | tf_op | source)
XLA Modules:
  0.0 143.6 jit_solution(12144771558275944027)
XLA Ops:
  0.6 1.8 %collective-permute-start = (bf16[512,1024]{1,0:T(8,128)(2,1)}, bf16[512,1024]{1,0:T(8,128)(2,1)S(1)}, u32[]{:S(2)}, u32[]{:S(2)}) collective-permute-start(bf16[512,1024]{1,0:T(8,128)(2,1)} %refs_0_.1), channel_id=1, source_target_pairs={{0,8},{1,33},{2,10},{3,35},{4,12},{5,37},{6,14},{7,39},{8,16},{9,4... | collective-permute-start | bytes 3145736 | tf_op jit(solution)/shard_map/ppermute | solution.py:278
  2.4 3.6 %merge.1 = (bf16[1152,512]{1,0:T(8,128)(2,1)}, bf16[192,512]{1,0:T(8,128)(2,1)}) custom-call(bf16[512,1024]{1,0:T(8,128)(2,1)} %refs_0_.1, bf16[64,512]{1,0:T(8,128)(2,1)} %bitcast.9, bf16[64,1024]{1,0:T(8,128)(2,1)} %high_ref.3, bf16[64,512]{1,0:T(8,128)(2,1)} %bitcast.10, bf16[64,512]{1,0:T(8,128)(2,1)} %bitcast.11, bf16[64,64]{1,0:T(8,128)(2,1)} %refs_5_.1, ...), custom_call_target="tpu_custom_call" | custom-call | flops 1000000000 | bytes 1 | tf_op jit(solution)/shard_map/merge/pallas_call | solution.py:64
  6.0 1.6 %collective-permute-start.1 = (bf16[192,512]{1,0:T(8,128)(2,1)}, bf16[192,512]{1,0:T(8,128)(2,1)S(1)}, u32[]{:S(2)}, u32[]{:S(2)}) collective-permute-start(bf16[192,512]{1,0:T(8,128)(2,1)} %get-tuple-element.36), channel_id=1, source_target_pairs={{0,8},{1,33},{2,10},{3,35},{4,12},{5,37},{6,14},{7,39},{8,16},{9,4... | collective-permute-start | bytes 589832 | tf_op jit(solution)/shard_map/ppermute | solution.py:278
  7.6 4.1 %collective-permute-start.10 = (bf16[1152,512]{1,0:T(8,128)(2,1)}, bf16[1152,512]{1,0:T(8,128)(2,1)S(1)}, u32[]{:S(2)}, u32[]{:S(2)}) collective-permute-start(bf16[1152,512]{1,0:T(8,128)(2,1)} %get-tuple-element.37.refs_0_), channel_id=1, source_target_pairs={{0,96},{1,25},{2,98},{3,27},{4,100},{5,29},{6,102},{7,31},{8,104},... | collective-permute-start | bytes 3538952 | tf_op jit(solution)/shard_map/ppermute | solution.py:281
  11.7 7.3 %collective-permute-done.1.side_ref = bf16[192,512]{1,0:T(8,128)(2,1)S(1)} collective-permute-done((bf16[192,512]{1,0:T(8,128)(2,1)}, bf16[192,512]{1,0:T(8,128)(2,1)S(1)}, u32[]{:S(2)}, u32[]{:S(2)}) %collective-permute-start.1) | collective-permute-done | bytes 196640 | tf_op jit(solution)/shard_map/ppermute | solution.py:278
  19.0 1.6 %finish.2.refs_0_ = bf16[1152,512]{1,0:T(8,128)(2,1)S(1)} custom-call(bf16[512,1024]{1,0:T(8,128)(2,1)S(1)} %collective-permute-done.train_ref, bf16[192,512]{1,0:T(8,128)(2,1)S(1)} %collective-permute-done.1.side_ref, bf16[64,1024]{1,0:T(8,128)(2,1)S(1)} %copy-done.1), custom_call_target="tpu_custom_call" | custom-call | flops 1000000000 | bytes 1 | tf_op jit(solution)/shard_map/finish/pallas_call | solution.py:102
  21.2 2.8 %collective-permute-start.12 = (bf16[512,1024]{1,0:T(8,128)(2,1)S(1)}, bf16[512,1024]{1,0:T(8,128)(2,1)S(1)}, u32[]{:S(2)}, u32[]{:S(2)}) collective-permute-start(bf16[512,1024]{1,0:T(8,128)(2,1)S(1)} %copy-done.2), channel_id=1, source_target_pairs={{0,24},{1,97},{2,26},{3,99},{4,28},{5,101},{6,30},{7,103},{8,0},{9... | collective-permute-start | bytes 3145736 | tf_op jit(solution)/shard_map/ppermute | solution.py:278
  24.0 0.7 collective-permute-start.13
  24.8 1.1 collective-permute-done.20.other_ref
  26.0 1.9 %collective-permute-start.21 = (f32[1,128]{1,0:T(1,128)S(1)}, f32[1,128]{1,0:T(1,128)S(1)}, u32[]{:S(2)}, u32[]{:S(2)}) collective-permute-start(f32[1,128]{1,0:T(1,128)S(1)} %join.7.mine_ref), channel_id=1, source_target_pairs={{0,32},{1,9},{2,34},{3,11},{4,36},{5,13},{6,38},{7,15},{8,40},{9,1... | collective-permute-start | bytes 1544 | tf_op jit(solution)/shard_map/ppermute | solution.py:223
  27.9 1.7 %collective-permute-done.21.other_ref = f32[1,128]{1,0:T(1,128)S(1)} collective-permute-done((f32[1,128]{1,0:T(1,128)S(1)}, f32[1,128]{1,0:T(1,128)S(1)}, u32[]{:S(2)}, u32[]{:S(2)}) %collective-permute-start.21) | collective-permute-done | bytes 544 | tf_op jit(solution)/shard_map/ppermute | solution.py:223
  29.6 3.9 %collective-permute-start.22 = (f32[2,128]{1,0:T(2,128)S(1)}, f32[2,128]{1,0:T(2,128)S(1)}, u32[]{:S(2)}, u32[]{:S(2)}) collective-permute-start(f32[2,128]{1,0:T(2,128)S(1)} %join.8.mine_ref), channel_id=1, source_target_pairs={{0,64},{1,17},{2,66},{3,19},{4,68},{5,21},{6,70},{7,23},{8,72},{9,... | collective-permute-start | bytes 3080 | tf_op jit(solution)/shard_map/ppermute | solution.py:223
  33.5 1.6 %collective-permute-done.22.other_ref = f32[2,128]{1,0:T(2,128)S(1)} collective-permute-done((f32[2,128]{1,0:T(2,128)S(1)}, f32[2,128]{1,0:T(2,128)S(1)}, u32[]{:S(2)}, u32[]{:S(2)}) %collective-permute-start.22) | collective-permute-done | bytes 1056 | tf_op jit(solution)/shard_map/ppermute | solution.py:223
  35.0 1.5 %collective-permute-start.23 = (f32[4,128]{1,0:T(4,128)S(1)}, f32[4,128]{1,0:T(4,128)S(1)}, u32[]{:S(2)}, u32[]{:S(2)}) collective-permute-start(f32[4,128]{1,0:T(4,128)S(1)} %join.9.mine_ref), channel_id=1, source_target_pairs={{0,2},{1,3},{2,0},{3,1},{4,6},{5,7},{6,4},{7,5},{8,10},{9,11},{10,... | collective-permute-start | bytes 6152 | tf_op jit(solution)/shard_map/ppermute | solution.py:223
  36.5 2.1 %collective-permute-done.23.other_ref = f32[4,128]{1,0:T(4,128)S(1)} collective-permute-done((f32[4,128]{1,0:T(4,128)S(1)}, f32[4,128]{1,0:T(4,128)S(1)}, u32[]{:S(2)}, u32[]{:S(2)}) %collective-permute-start.23) | collective-permute-done | bytes 2080 | tf_op jit(solution)/shard_map/ppermute | solution.py:223
  38.6 3.0 %collective-permute-start.24 = (f32[8,128]{1,0:T(8,128)S(1)}, f32[8,128]{1,0:T(8,128)S(1)}, u32[]{:S(2)}, u32[]{:S(2)}) collective-permute-start(f32[8,128]{1,0:T(8,128)S(1)} %join.10.mine_ref), channel_id=1, source_target_pairs={{0,4},{1,5},{2,6},{3,7},{4,0},{5,1},{6,2},{7,3},{8,12},{9,13},{10,... | collective-permute-start | bytes 12296 | tf_op jit(solution)/shard_map/ppermute | solution.py:223
  41.6 2.1 %collective-permute-done.24.other_ref = f32[8,128]{1,0:T(8,128)S(1)} collective-permute-done((f32[8,128]{1,0:T(8,128)S(1)}, f32[8,128]{1,0:T(8,128)S(1)}, u32[]{:S(2)}, u32[]{:S(2)}) %collective-permute-start.24) | collective-permute-done | bytes 4128 | tf_op jit(solution)/shard_map/ppermute | solution.py:223
  43.7 1.4 %collective-permute-start.25 = (f32[16,128]{1,0:T(8,128)S(1)}, f32[16,128]{1,0:T(8,128)S(1)}, u32[]{:S(2)}, u32[]{:S(2)}) collective-permute-start(f32[16,128]{1,0:T(8,128)S(1)} %join.11.mine_ref), channel_id=1, source_target_pairs={{0,8},{1,33},{2,10},{3,35},{4,12},{5,37},{6,14},{7,39},{8,0},{9,41... | collective-permute-start | bytes 24584 | tf_op jit(solution)/shard_map/ppermute | solution.py:223
  45.2 2.2 %collective-permute-done.25.other_ref = f32[16,128]{1,0:T(8,128)S(1)} collective-permute-done((f32[16,128]{1,0:T(8,128)S(1)}, f32[16,128]{1,0:T(8,128)S(1)}, u32[]{:S(2)}, u32[]{:S(2)}) %collective-permute-start.25) | collective-permute-done | bytes 8224 | tf_op jit(solution)/shard_map/ppermute | solution.py:223
  47.4 1.7 %collective-permute-start.26 = (f32[32,128]{1,0:T(8,128)S(1)}, f32[32,128]{1,0:T(8,128)S(1)}, u32[]{:S(2)}, u32[]{:S(2)}) collective-permute-start(f32[32,128]{1,0:T(8,128)S(1)} %join.12.mine_ref), channel_id=1, source_target_pairs={{0,16},{1,65},{2,18},{3,67},{4,20},{5,69},{6,22},{7,71},{8,24},{9,... | collective-permute-start | bytes 49160 | tf_op jit(solution)/shard_map/ppermute | solution.py:223
  49.0 3.8 %collective-permute-done.26.other_ref = f32[32,128]{1,0:T(8,128)S(1)} collective-permute-done((f32[32,128]{1,0:T(8,128)S(1)}, f32[32,128]{1,0:T(8,128)S(1)}, u32[]{:S(2)}, u32[]{:S(2)}) %collective-permute-start.26) | collective-permute-done | bytes 16416 | tf_op jit(solution)/shard_map/ppermute | solution.py:223
  52.8 1.6 %collective-permute-start.19 = (bf16[1152,512]{1,0:T(8,128)(2,1)S(1)}, bf16[1152,512]{1,0:T(8,128)(2,1)S(1)}, u32[]{:S(2)}, u32[]{:S(2)}) collective-permute-start(bf16[1152,512]{1,0:T(8,128)(2,1)S(1)} %copy-done), channel_id=1, source_target_pairs={{0,32},{1,9},{2,34},{3,11},{4,36},{5,13},{6,38},{7,15},{8,40},{9,1... | collective-permute-start | bytes 3538952 | tf_op jit(solution)/shard_map/ppermute | solution.py:281
  54.4 2.2 %collective-permute-start.2 = (bf16[1152,512]{1,0:T(8,128)(2,1)S(1)}, bf16[1152,512]{1,0:T(8,128)(2,1)S(1)}, u32[]{:S(2)}, u32[]{:S(2)}) collective-permute-start(bf16[1152,512]{1,0:T(8,128)(2,1)S(1)} %finish.2.refs_0_), channel_id=1, source_target_pairs={{0,96},{1,25},{2,98},{3,27},{4,100},{5,29},{6,102},{7,31},{8,104},... | collective-permute-start | bytes 3538952 | tf_op jit(solution)/shard_map/ppermute | solution.py:281
  56.6 1.6 %finish.3.refs_1_ = bf16[1152,512]{1,0:T(8,128)(2,1)S(1)} custom-call(bf16[512,1024]{1,0:T(8,128)(2,1)S(1)} %collective-permute-done.12.train_ref, bf16[192,512]{1,0:T(8,128)(2,1)S(1)} %collective-permute-done.13.side_ref, bf16[64,1024]{1,0:T(8,128)(2,1)S(1)} %copy-done.1), custom_call_target="tpu_custom_call" | custom-call | flops 1000000000 | bytes 1 | tf_op jit(solution)/shard_map/finish/pallas_call | solution.py:102
  58.2 1.8 %collective-permute-start.14 = (bf16[1152,512]{1,0:T(8,128)(2,1)S(1)}, bf16[1152,512]{1,0:T(8,128)(2,1)S(1)}, u32[]{:S(2)}, u32[]{:S(2)}) collective-permute-start(bf16[1152,512]{1,0:T(8,128)(2,1)S(1)} %finish.3.refs_1_), channel_id=1, source_target_pairs={{0,32},{1,9},{2,34},{3,11},{4,36},{5,13},{6,38},{7,15},{8,40},{9,1... | collective-permute-start | bytes 3538952 | tf_op jit(solution)/shard_map/ppermute | solution.py:281
  60.0 1.6 %collective-permute-start.7 = (bf16[1152,512]{1,0:T(8,128)(2,1)S(1)}, bf16[1152,512]{1,0:T(8,128)(2,1)S(1)}, u32[]{:S(2)}, u32[]{:S(2)}) collective-permute-start(bf16[1152,512]{1,0:T(8,128)(2,1)S(1)} %collective-permute-done.6.refs_0_), channel_id=1, source_target_pairs={{0,96},{1,25},{2,98},{3,27},{4,100},{5,29},{6,102},{7,31},{8,104},... | collective-permute-start | bytes 3538952 | tf_op jit(solution)/shard_map/ppermute | solution.py:281
  61.6 9.1 %collective-permute-done.19.refs_0_ = bf16[1152,512]{1,0:T(8,128)(2,1)S(1)} collective-permute-done((bf16[1152,512]{1,0:T(8,128)(2,1)S(1)}, bf16[1152,512]{1,0:T(8,128)(2,1)S(1)}, u32[]{:S(2)}, u32[]{:S(2)}) %collective-permute-start.19) | collective-permute-done | bytes 1179680 | tf_op jit(solution)/shard_map/ppermute | solution.py:281
  70.7 2.0 %collective-permute-start.18 = (bf16[1152,512]{1,0:T(8,128)(2,1)S(1)}, bf16[1152,512]{1,0:T(8,128)(2,1)S(1)}, u32[]{:S(2)}, u32[]{:S(2)}) collective-permute-start(bf16[1152,512]{1,0:T(8,128)(2,1)S(1)} %finish.3.refs_1_), channel_id=1, source_target_pairs={{0,96},{1,25},{2,98},{3,27},{4,100},{5,29},{6,102},{7,31},{8,104},... | collective-permute-start | bytes 3538952 | tf_op jit(solution)/shard_map/ppermute | solution.py:281
  72.7 1.3 collective-permute-start.11
  74.0 9.3 %collective-permute-done.4.refs_0_ = bf16[1152,512]{1,0:T(8,128)(2,1)S(1)} collective-permute-done((bf16[1152,512]{1,0:T(8,128)(2,1)S(1)}, bf16[1152,512]{1,0:T(8,128)(2,1)S(1)}, u32[]{:S(2)}, u32[]{:S(2)}) %collective-permute-start.4) | collective-permute-done | bytes 1179680 | tf_op jit(solution)/shard_map/ppermute | solution.py:281
  83.3 12.6 %collective-permute-done.14.refs_0_ = bf16[1152,512]{1,0:T(8,128)(2,1)S(1)} collective-permute-done((bf16[1152,512]{1,0:T(8,128)(2,1)S(1)}, bf16[1152,512]{1,0:T(8,128)(2,1)S(1)}, u32[]{:S(2)}, u32[]{:S(2)}) %collective-permute-start.14) | collective-permute-done | bytes 1179680 | tf_op jit(solution)/shard_map/ppermute | solution.py:281
  96.0 3.2 %collective-permute-start.8 = (bf16[1152,512]{1,0:T(8,128)(2,1)S(1)}, bf16[1152,512]{1,0:T(8,128)(2,1)S(1)}, u32[]{:S(2)}, u32[]{:S(2)}) collective-permute-start(bf16[1152,512]{1,0:T(8,128)(2,1)S(1)} %collective-permute-done.7.refs_1_), channel_id=1, source_target_pairs={{0,96},{1,25},{2,98},{3,27},{4,100},{5,29},{6,102},{7,31},{8,104},... | collective-permute-start | bytes 3538952 | tf_op jit(solution)/shard_map/ppermute | solution.py:281
  99.2 0.9 collective-permute-start.17
  100.2 8.3 %collective-permute-done.11.refs_0_ = bf16[1152,512]{1,0:T(8,128)(2,1)S(1)} collective-permute-done((bf16[1152,512]{1,0:T(8,128)(2,1)S(1)}, bf16[1152,512]{1,0:T(8,128)(2,1)S(1)}, u32[]{:S(2)}, u32[]{:S(2)}) %collective-permute-start.11) | collective-permute-done | bytes 1179680 | tf_op jit(solution)/shard_map/ppermute | solution.py:281
  108.5 1.9 %collective-permute-start.9 = (bf16[480,512]{1,0:T(8,128)(2,1)S(1)}, bf16[480,512]{1,0:T(8,128)(2,1)S(1)}, u32[]{:S(2)}, u32[]{:S(2)}) collective-permute-start(bf16[480,512]{1,0:T(8,128)(2,1)S(1)} %slice.18), channel_id=1, source_target_pairs={{0,32},{1,9},{2,34},{3,11},{4,36},{5,13},{6,38},{7,15},{8,40},{9,1... | collective-permute-start | bytes 1474568 | tf_op jit(solution)/shard_map/ppermute | solution.py:281
  110.4 15.3 %collective-permute-done.17.refs_1_ = bf16[416,512]{1,0:T(8,128)(2,1)S(1)} collective-permute-done((bf16[416,512]{1,0:T(8,128)(2,1)S(1)}, bf16[416,512]{1,0:T(8,128)(2,1)S(1)}, u32[]{:S(2)}, u32[]{:S(2)}) %collective-permute-start.17) | collective-permute-done | bytes 426016 | tf_op jit(solution)/shard_map/ppermute | solution.py:281
  125.7 3.4 %collective-permute-start.3 = (bf16[128,512]{1,0:T(8,128)(2,1)S(1)}, bf16[128,512]{1,0:T(8,128)(2,1)S(1)}, u32[]{:S(2)}, u32[]{:S(2)}) collective-permute-start(bf16[128,512]{1,0:T(8,128)(2,1)S(1)} %slice.16), channel_id=1, source_target_pairs={{0,96},{1,25},{2,98},{3,27},{4,100},{5,29},{6,102},{7,31},{8,104},... | collective-permute-start | bytes 393224 | tf_op jit(solution)/shard_map/ppermute | solution.py:281
  129.1 1.3 place.10
  130.4 0.8 order.1
  131.2 1.5 %place.11 = (bf16[1024,8192]{1,0:T(8,128)(2,1)}, bf16[64,8192]{1,0:T(8,128)(2,1)}, bf16[64,8192]{1,0:T(8,128)(2,1)}) custom-call(bf16[1152,512]{1,0:T(8,128)(2,1)S(1)} %collective-permute-done.19.refs_0_, bf16[1152,512]{1,0:T(8,128)(2,1)S(1)} %collective-permute-done.10.refs_1_, ...), custom_call_target="tpu_custom_call", output_to_operand_aliasing={{0}: (2, {}), {1}: (3, {}), {2}: (4, {})} | custom-call | flops 1000000 | bytes 4718592 | tf_op jit(solution)/shard_map/place/pallas_call | solution.py:166
  132.6 1.5 %place.12 = (bf16[1024,8192]{1,0:T(8,128)(2,1)}, bf16[64,8192]{1,0:T(8,128)(2,1)}, bf16[64,8192]{1,0:T(8,128)(2,1)}) custom-call(bf16[1152,512]{1,0:T(8,128)(2,1)S(1)} %finish.2.refs_0_, bf16[1152,512]{1,0:T(8,128)(2,1)S(1)} %finish.3.refs_1_, ...), custom_call_target="tpu_custom_call", output_to_operand_aliasing={{0}: (2, {}), {1}: (3, {}), {2}: (4, {})} | custom-call | flops 1000000 | bytes 4718592 | tf_op jit(solution)/shard_map/place/pallas_call | solution.py:166
  134.2 1.5 %place.13 = (bf16[1024,8192]{1,0:T(8,128)(2,1)}, bf16[64,8192]{1,0:T(8,128)(2,1)}, bf16[64,8192]{1,0:T(8,128)(2,1)}) custom-call(bf16[1152,512]{1,0:T(8,128)(2,1)S(1)} %collective-permute-done.6.refs_0_, bf16[1152,512]{1,0:T(8,128)(2,1)S(1)} %collective-permute-done.2.refs_1_, ...), custom_call_target="tpu_custom_call", output_to_operand_aliasing={{0}: (2, {}), {1}: (3, {}), {2}: (4, {})} | custom-call | flops 1000000 | bytes 4718592 | tf_op jit(solution)/shard_map/place/pallas_call | solution.py:166
  135.7 1.5 %place.14 = (bf16[1024,8192]{1,0:T(8,128)(2,1)}, bf16[64,8192]{1,0:T(8,128)(2,1)}, bf16[64,8192]{1,0:T(8,128)(2,1)}) custom-call(bf16[1152,512]{1,0:T(8,128)(2,1)S(1)} %collective-permute-done.4.refs_0_, bf16[1152,512]{1,0:T(8,128)(2,1)S(1)} %collective-permute-done.18.refs_1_, ...), custom_call_target="tpu_custom_call", output_to_operand_aliasing={{0}: (2, {}), {1}: (3, {}), {2}: (4, {})} | custom-call | flops 1000000 | bytes 4718592 | tf_op jit(solution)/shard_map/place/pallas_call | solution.py:166
  137.2 1.3 place.15
  138.4 1.5 %place.16 = (bf16[1024,8192]{1,0:T(8,128)(2,1)}, bf16[64,8192]{1,0:T(8,128)(2,1)}, bf16[64,8192]{1,0:T(8,128)(2,1)}) custom-call(bf16[1152,512]{1,0:T(8,128)(2,1)S(1)} %collective-permute-done.16.refs_0_, bf16[1152,512]{1,0:T(8,128)(2,1)S(1)} %collective-permute-done.7.refs_1_, ...), custom_call_target="tpu_custom_call", output_to_operand_aliasing={{0}: (2, {}), {1}: (3, {}), {2}: (4, {})} | custom-call | flops 1000000 | bytes 4718592 | tf_op jit(solution)/shard_map/place/pallas_call | solution.py:166
  140.0 1.5 %place.17 = (bf16[1024,8192]{1,0:T(8,128)(2,1)}, bf16[64,8192]{1,0:T(8,128)(2,1)}, bf16[64,8192]{1,0:T(8,128)(2,1)}) custom-call(bf16[1152,512]{1,0:T(8,128)(2,1)S(1)} %collective-permute-done.11.refs_0_, bf16[1152,512]{1,0:T(8,128)(2,1)S(1)} %collective-permute-done.15.refs_1_, ...), custom_call_target="tpu_custom_call", output_to_operand_aliasing={{0}: (2, {}), {1}: (3, {}), {2}: (4, {})} | custom-call | flops 1000000 | bytes 4718592 | tf_op jit(solution)/shard_map/place/pallas_call | solution.py:166
  141.5 1.3 place.18
  142.8 0.8 place.19
  (44 shorter events, 0.9 us)
Async XLA Ops:
  0.6 18.4 %collective-permute-start = (bf16[512,1024]{1,0:T(8,128)(2,1)}, bf16[512,1024]{1,0:T(8,128)(2,1)S(1)}, u32[]{:S(2)}, u32[]{:S(2)}) collective-permute-start(bf16[512,1024]{1,0:T(8,128)(2,1)} %refs_0_.1), channel_id=1, source_target_pairs={{0,8},{1,33},{2,10},{3,35},{4,12},{5,37},{6,14},{7,39},{8,16},{9,4... | collective-permute-start | bytes 3145736 | tf_op jit(solution)/shard_map/ppermute | solution.py:278
  2.4 16.6 %copy-start.1 = (bf16[64,1024]{1,0:T(8,128)(2,1)S(1)}, bf16[64,1024]{1,0:T(8,128)(2,1)}, u32[]{:S(2)}) copy-start(bf16[64,1024]{1,0:T(8,128)(2,1)} %high_ref.3) | copy-start | bytes 393220
  6.0 13.1 %collective-permute-start.1 = (bf16[192,512]{1,0:T(8,128)(2,1)}, bf16[192,512]{1,0:T(8,128)(2,1)S(1)}, u32[]{:S(2)}, u32[]{:S(2)}) collective-permute-start(bf16[192,512]{1,0:T(8,128)(2,1)} %get-tuple-element.36), channel_id=1, source_target_pairs={{0,8},{1,33},{2,10},{3,35},{4,12},{5,37},{6,14},{7,39},{8,16},{9,4... | collective-permute-start | bytes 589832 | tf_op jit(solution)/shard_map/ppermute | solution.py:278
  7.6 13.6 %copy-start.2 = (bf16[512,1024]{1,0:T(8,128)(2,1)S(1)}, bf16[512,1024]{1,0:T(8,128)(2,1)}, u32[]{:S(2)}) copy-start(bf16[512,1024]{1,0:T(8,128)(2,1)} %refs_0_.1) | copy-start | bytes 3145732
  7.6 16.4 %copy-start.3 = (bf16[192,512]{1,0:T(8,128)(2,1)S(1)}, bf16[192,512]{1,0:T(8,128)(2,1)}, u32[]{:S(2)}) copy-start(bf16[192,512]{1,0:T(8,128)(2,1)} %get-tuple-element.36) | copy-start | bytes 589828
  7.6 17.1 %copy-start.4 = (f32[64]{0:T(128)S(1)}, f32[64]{0:T(128)}, u32[]{:S(2)}) copy-start(f32[64]{0:T(128)} %param.20) | copy-start | bytes 772
  7.6 17.1 %copy-start.5 = (f32[64]{0:T(128)S(1)}, f32[64]{0:T(128)}, u32[]{:S(2)}) copy-start(f32[64]{0:T(128)} %param.21) | copy-start | bytes 772
  7.6 45.2 %copy-start = (bf16[1152,512]{1,0:T(8,128)(2,1)S(1)}, bf16[1152,512]{1,0:T(8,128)(2,1)}, u32[]{:S(2)}) copy-start(bf16[1152,512]{1,0:T(8,128)(2,1)} %get-tuple-element.37.refs_0_) | copy-start | bytes 3538948
  7.6 50.6 %collective-permute-start.10 = (bf16[1152,512]{1,0:T(8,128)(2,1)}, bf16[1152,512]{1,0:T(8,128)(2,1)S(1)}, u32[]{:S(2)}, u32[]{:S(2)}) collective-permute-start(bf16[1152,512]{1,0:T(8,128)(2,1)} %get-tuple-element.37.refs_0_), channel_id=1, source_target_pairs={{0,96},{1,25},{2,98},{3,27},{4,100},{5,29},{6,102},{7,31},{8,104},... | collective-permute-start | bytes 3538952 | tf_op jit(solution)/shard_map/ppermute | solution.py:281
  20.7 39.3 %collective-permute-start.6 = (bf16[1152,512]{1,0:T(8,128)(2,1)S(1)}, bf16[1152,512]{1,0:T(8,128)(2,1)S(1)}, u32[]{:S(2)}, u32[]{:S(2)}) collective-permute-start(bf16[1152,512]{1,0:T(8,128)(2,1)S(1)} %finish.2.refs_0_), channel_id=1, source_target_pairs={{0,8},{1,33},{2,10},{3,35},{4,12},{5,37},{6,14},{7,39},{8,16},{9,4... | collective-permute-start | bytes 3538952 | tf_op jit(solution)/shard_map/ppermute | solution.py:278
  21.2 35.4 %collective-permute-start.12 = (bf16[512,1024]{1,0:T(8,128)(2,1)S(1)}, bf16[512,1024]{1,0:T(8,128)(2,1)S(1)}, u32[]{:S(2)}, u32[]{:S(2)}) collective-permute-start(bf16[512,1024]{1,0:T(8,128)(2,1)S(1)} %copy-done.2), channel_id=1, source_target_pairs={{0,24},{1,97},{2,26},{3,99},{4,28},{5,101},{6,30},{7,103},{8,0},{9... | collective-permute-start | bytes 3145736 | tf_op jit(solution)/shard_map/ppermute | solution.py:278
  24.0 30.4 %collective-permute-start.13 = (bf16[192,512]{1,0:T(8,128)(2,1)S(1)}, bf16[192,512]{1,0:T(8,128)(2,1)S(1)}, u32[]{:S(2)}, u32[]{:S(2)}) collective-permute-start(bf16[192,512]{1,0:T(8,128)(2,1)S(1)} %copy-done.3), channel_id=1, source_target_pairs={{0,24},{1,97},{2,26},{3,99},{4,28},{5,101},{6,30},{7,103},{8,0},{9... | collective-permute-start | bytes 589832 | tf_op jit(solution)/shard_map/ppermute | solution.py:278
  24.7 1.2 collective-permute-start.20
  26.0 3.6 %collective-permute-start.21 = (f32[1,128]{1,0:T(1,128)S(1)}, f32[1,128]{1,0:T(1,128)S(1)}, u32[]{:S(2)}, u32[]{:S(2)}) collective-permute-start(f32[1,128]{1,0:T(1,128)S(1)} %join.7.mine_ref), channel_id=1, source_target_pairs={{0,32},{1,9},{2,34},{3,11},{4,36},{5,13},{6,38},{7,15},{8,40},{9,1... | collective-permute-start | bytes 1544 | tf_op jit(solution)/shard_map/ppermute | solution.py:223
  29.6 5.4 %collective-permute-start.22 = (f32[2,128]{1,0:T(2,128)S(1)}, f32[2,128]{1,0:T(2,128)S(1)}, u32[]{:S(2)}, u32[]{:S(2)}) collective-permute-start(f32[2,128]{1,0:T(2,128)S(1)} %join.8.mine_ref), channel_id=1, source_target_pairs={{0,64},{1,17},{2,66},{3,19},{4,68},{5,21},{6,70},{7,23},{8,72},{9,... | collective-permute-start | bytes 3080 | tf_op jit(solution)/shard_map/ppermute | solution.py:223
  35.0 3.6 %collective-permute-start.23 = (f32[4,128]{1,0:T(4,128)S(1)}, f32[4,128]{1,0:T(4,128)S(1)}, u32[]{:S(2)}, u32[]{:S(2)}) collective-permute-start(f32[4,128]{1,0:T(4,128)S(1)} %join.9.mine_ref), channel_id=1, source_target_pairs={{0,2},{1,3},{2,0},{3,1},{4,6},{5,7},{6,4},{7,5},{8,10},{9,11},{10,... | collective-permute-start | bytes 6152 | tf_op jit(solution)/shard_map/ppermute | solution.py:223
  38.6 5.1 %collective-permute-start.24 = (f32[8,128]{1,0:T(8,128)S(1)}, f32[8,128]{1,0:T(8,128)S(1)}, u32[]{:S(2)}, u32[]{:S(2)}) collective-permute-start(f32[8,128]{1,0:T(8,128)S(1)} %join.10.mine_ref), channel_id=1, source_target_pairs={{0,4},{1,5},{2,6},{3,7},{4,0},{5,1},{6,2},{7,3},{8,12},{9,13},{10,... | collective-permute-start | bytes 12296 | tf_op jit(solution)/shard_map/ppermute | solution.py:223
  43.7 3.7 %collective-permute-start.25 = (f32[16,128]{1,0:T(8,128)S(1)}, f32[16,128]{1,0:T(8,128)S(1)}, u32[]{:S(2)}, u32[]{:S(2)}) collective-permute-start(f32[16,128]{1,0:T(8,128)S(1)} %join.11.mine_ref), channel_id=1, source_target_pairs={{0,8},{1,33},{2,10},{3,35},{4,12},{5,37},{6,14},{7,39},{8,0},{9,41... | collective-permute-start | bytes 24584 | tf_op jit(solution)/shard_map/ppermute | solution.py:223
  47.4 5.4 %collective-permute-start.26 = (f32[32,128]{1,0:T(8,128)S(1)}, f32[32,128]{1,0:T(8,128)S(1)}, u32[]{:S(2)}, u32[]{:S(2)}) collective-permute-start(f32[32,128]{1,0:T(8,128)S(1)} %join.12.mine_ref), channel_id=1, source_target_pairs={{0,16},{1,65},{2,18},{3,67},{4,20},{5,69},{6,22},{7,71},{8,24},{9,... | collective-permute-start | bytes 49160 | tf_op jit(solution)/shard_map/ppermute | solution.py:223
  52.8 17.9 %collective-permute-start.19 = (bf16[1152,512]{1,0:T(8,128)(2,1)S(1)}, bf16[1152,512]{1,0:T(8,128)(2,1)S(1)}, u32[]{:S(2)}, u32[]{:S(2)}) collective-permute-start(bf16[1152,512]{1,0:T(8,128)(2,1)S(1)} %copy-done), channel_id=1, source_target_pairs={{0,32},{1,9},{2,34},{3,11},{4,36},{5,13},{6,38},{7,15},{8,40},{9,1... | collective-permute-start | bytes 3538952 | tf_op jit(solution)/shard_map/ppermute | solution.py:281
  54.4 18.3 %collective-permute-start.2 = (bf16[1152,512]{1,0:T(8,128)(2,1)S(1)}, bf16[1152,512]{1,0:T(8,128)(2,1)S(1)}, u32[]{:S(2)}, u32[]{:S(2)}) collective-permute-start(bf16[1152,512]{1,0:T(8,128)(2,1)S(1)} %finish.2.refs_0_), channel_id=1, source_target_pairs={{0,96},{1,25},{2,98},{3,27},{4,100},{5,29},{6,102},{7,31},{8,104},... | collective-permute-start | bytes 3538952 | tf_op jit(solution)/shard_map/ppermute | solution.py:281
  56.6 26.7 %collective-permute-start.4 = (bf16[1152,512]{1,0:T(8,128)(2,1)S(1)}, bf16[1152,512]{1,0:T(8,128)(2,1)S(1)}, u32[]{:S(2)}, u32[]{:S(2)}) collective-permute-start(bf16[1152,512]{1,0:T(8,128)(2,1)S(1)} %finish.2.refs_0_), channel_id=1, source_target_pairs={{0,32},{1,9},{2,34},{3,11},{4,36},{5,13},{6,38},{7,15},{8,40},{9,1... | collective-permute-start | bytes 3538952 | tf_op jit(solution)/shard_map/ppermute | solution.py:281
  58.2 37.7 %collective-permute-start.14 = (bf16[1152,512]{1,0:T(8,128)(2,1)S(1)}, bf16[1152,512]{1,0:T(8,128)(2,1)S(1)}, u32[]{:S(2)}, u32[]{:S(2)}) collective-permute-start(bf16[1152,512]{1,0:T(8,128)(2,1)S(1)} %finish.3.refs_1_), channel_id=1, source_target_pairs={{0,32},{1,9},{2,34},{3,11},{4,36},{5,13},{6,38},{7,15},{8,40},{9,1... | collective-permute-start | bytes 3538952 | tf_op jit(solution)/shard_map/ppermute | solution.py:281
  60.0 36.0 %collective-permute-start.7 = (bf16[1152,512]{1,0:T(8,128)(2,1)S(1)}, bf16[1152,512]{1,0:T(8,128)(2,1)S(1)}, u32[]{:S(2)}, u32[]{:S(2)}) collective-permute-start(bf16[1152,512]{1,0:T(8,128)(2,1)S(1)} %collective-permute-done.6.refs_0_), channel_id=1, source_target_pairs={{0,96},{1,25},{2,98},{3,27},{4,100},{5,29},{6,102},{7,31},{8,104},... | collective-permute-start | bytes 3538952 | tf_op jit(solution)/shard_map/ppermute | solution.py:281
  70.7 28.6 %collective-permute-start.18 = (bf16[1152,512]{1,0:T(8,128)(2,1)S(1)}, bf16[1152,512]{1,0:T(8,128)(2,1)S(1)}, u32[]{:S(2)}, u32[]{:S(2)}) collective-permute-start(bf16[1152,512]{1,0:T(8,128)(2,1)S(1)} %finish.3.refs_1_), channel_id=1, source_target_pairs={{0,96},{1,25},{2,98},{3,27},{4,100},{5,29},{6,102},{7,31},{8,104},... | collective-permute-start | bytes 3538952 | tf_op jit(solution)/shard_map/ppermute | solution.py:281
  72.7 35.8 %collective-permute-start.11 = (bf16[1152,512]{1,0:T(8,128)(2,1)S(1)}, bf16[1152,512]{1,0:T(8,128)(2,1)S(1)}, u32[]{:S(2)}, u32[]{:S(2)}) collective-permute-start(bf16[1152,512]{1,0:T(8,128)(2,1)S(1)} %collective-permute-done.10.refs_1_), channel_id=1, source_target_pairs={{0,96},{1,25},{2,98},{3,27},{4,100},{5,29},{6,102},{7,31},{8,104},... | collective-permute-start | bytes 3538952 | tf_op jit(solution)/shard_map/ppermute | solution.py:281
  83.3 45.8 %collective-permute-start.16 = (bf16[1152,512]{1,0:T(8,128)(2,1)S(1)}, bf16[1152,512]{1,0:T(8,128)(2,1)S(1)}, u32[]{:S(2)}, u32[]{:S(2)}) collective-permute-start(bf16[1152,512]{1,0:T(8,128)(2,1)S(1)} %collective-permute-done.6.refs_0_), channel_id=1, source_target_pairs={{0,32},{1,9},{2,34},{3,11},{4,36},{5,13},{6,38},{7,15},{8,40},{9,1... | collective-permute-start | bytes 3538952 | tf_op jit(solution)/shard_map/ppermute | solution.py:281
  96.0 44.0 %collective-permute-start.15 = (bf16[1152,512]{1,0:T(8,128)(2,1)S(1)}, bf16[1152,512]{1,0:T(8,128)(2,1)S(1)}, u32[]{:S(2)}, u32[]{:S(2)}) collective-permute-start(bf16[1152,512]{1,0:T(8,128)(2,1)S(1)} %collective-permute-done.14.refs_0_), channel_id=1, source_target_pairs={{0,32},{1,9},{2,34},{3,11},{4,36},{5,13},{6,38},{7,15},{8,40},{9,1... | collective-permute-start | bytes 3538952 | tf_op jit(solution)/shard_map/ppermute | solution.py:281
  96.0 45.5 %collective-permute-start.8 = (bf16[1152,512]{1,0:T(8,128)(2,1)S(1)}, bf16[1152,512]{1,0:T(8,128)(2,1)S(1)}, u32[]{:S(2)}, u32[]{:S(2)}) collective-permute-start(bf16[1152,512]{1,0:T(8,128)(2,1)S(1)} %collective-permute-done.7.refs_1_), channel_id=1, source_target_pairs={{0,96},{1,25},{2,98},{3,27},{4,100},{5,29},{6,102},{7,31},{8,104},... | collective-permute-start | bytes 3538952 | tf_op jit(solution)/shard_map/ppermute | solution.py:281
  99.2 26.5 %collective-permute-start.17 = (bf16[416,512]{1,0:T(8,128)(2,1)S(1)}, bf16[416,512]{1,0:T(8,128)(2,1)S(1)}, u32[]{:S(2)}, u32[]{:S(2)}) collective-permute-start(bf16[416,512]{1,0:T(8,128)(2,1)S(1)} %slice.19), channel_id=1, source_target_pairs={{0,96},{1,25},{2,98},{3,27},{4,100},{5,29},{6,102},{7,31},{8,104},... | collective-permute-start | bytes 1277960 | tf_op jit(solution)/shard_map/ppermute | solution.py:281
  108.5 33.0 %collective-permute-start.9 = (bf16[480,512]{1,0:T(8,128)(2,1)S(1)}, bf16[480,512]{1,0:T(8,128)(2,1)S(1)}, u32[]{:S(2)}, u32[]{:S(2)}) collective-permute-start(bf16[480,512]{1,0:T(8,128)(2,1)S(1)} %slice.18), channel_id=1, source_target_pairs={{0,32},{1,9},{2,34},{3,11},{4,36},{5,13},{6,38},{7,15},{8,40},{9,1... | collective-permute-start | bytes 1474568 | tf_op jit(solution)/shard_map/ppermute | solution.py:281
  125.7 17.1 %collective-permute-start.3 = (bf16[128,512]{1,0:T(8,128)(2,1)S(1)}, bf16[128,512]{1,0:T(8,128)(2,1)S(1)}, u32[]{:S(2)}, u32[]{:S(2)}) collective-permute-start(bf16[128,512]{1,0:T(8,128)(2,1)S(1)} %slice.16), channel_id=1, source_target_pairs={{0,96},{1,25},{2,98},{3,27},{4,100},{5,29},{6,102},{7,31},{8,104},... | collective-permute-start | bytes 393224 | tf_op jit(solution)/shard_map/ppermute | solution.py:281
  129.1 13.7 %collective-permute-start.5 = (bf16[128,512]{1,0:T(8,128)(2,1)S(1)}, bf16[128,512]{1,0:T(8,128)(2,1)S(1)}, u32[]{:S(2)}, u32[]{:S(2)}) collective-permute-start(bf16[128,512]{1,0:T(8,128)(2,1)S(1)} %slice.17), channel_id=1, source_target_pairs={{0,32},{1,9},{2,34},{3,11},{4,36},{5,13},{6,38},{7,15},{8,40},{9,1... | collective-permute-start | bytes 393224 | tf_op jit(solution)/shard_map/ppermute | solution.py:281
